TPU v7x, 16 devices: a whole 2x2x2 slice. The times are simulated.
16 devices in a mesh: ty: 2 (over z), tx: 8 (over y, x, core).
Axes of the slice: x: 2, y: 2, z: 2, core: 2. Of those that a mesh axis runs over, the one named last changes fastest.
Arguments:
- x_tok: bfloat16 [256, 4096], P('ty', 'tx')
- dy_tok: bfloat16 [256, 4096], P('ty', 'tx')
- ln_gain: float32 [4096], P('tx')
- w_gate: bfloat16 [4096, 16384], P('tx', 'ty')
- w_up: bfloat16 [4096, 16384], P('tx', 'ty')
- w_down: bfloat16 [16384, 4096], P('ty', 'tx')
Outputs:
- output 1: bfloat16 [256, 4096], P('ty', 'tx')
- output 2: bfloat16 [256, 4096], P('ty', 'tx')
- output 3: float32 [4096, 16384], P('tx', 'ty')
- output 4: float32 [4096, 16384], P('tx', 'ty')
- output 5: float32 [16384, 4096], P('ty', 'tx')
- output 6: float32 [4096], P('tx')
All inputs are finite; a program needn't handle non-finite values.
Results may differ from a plain program's by a relative error of at most 0.00184539.
Values are sent between devices in bfloat16 or wider.
A program may use at most 1 GiB of HBM per device.

v0:
```python
import jax
import jax.numpy as jnp
from jax import lax
from jax.sharding import PartitionSpec as P

LN_EPS = 1e-6


def contract_rows(left_op, right_op):
    return lax.dot_general(left_op, right_op, (((0,), (0,)), ((), ())), preferred_element_type=jnp.float32)


def contract_cols(left_op, right_op):
    return lax.dot_general(left_op, right_op, (((1,), (1,)), ((), ())), preferred_element_type=jnp.float32)


def solution(mesh):
    tx_size = mesh.shape["tx"]

    def local_step(x_blk, dy_blk, gain_blk, w_gate_blk, w_up_blk, w_down_blk):
        d_model = x_blk.shape[1] * tx_size
        x_float = x_blk.astype(jnp.float32)
        ln_stats = lax.psum(jnp.stack([jnp.sum(x_float, axis=1), jnp.sum(x_float * x_float, axis=1)]), "tx") / d_model
        mean_x = ln_stats[0][:, None]
        inv_std = lax.rsqrt(ln_stats[1][:, None] - mean_x * mean_x + LN_EPS)
        x_hat = (x_float - mean_x) * inv_std
        h_blk = (gain_blk * x_hat).astype(jnp.bfloat16)
        h_all = lax.all_gather(h_blk, "ty", axis=0, tiled=True)
        gate_pre = lax.psum_scatter(jnp.dot(h_all, w_gate_blk, preferred_element_type=jnp.float32),
                                    "tx", scatter_dimension=0, tiled=True)
        up_pre = lax.psum_scatter(jnp.dot(h_all, w_up_blk, preferred_element_type=jnp.float32),
                                  "tx", scatter_dimension=0, tiled=True)
        gate_sig = jax.nn.sigmoid(gate_pre)
        gate_swish = gate_pre * gate_sig
        act_blk = (gate_swish * up_pre).astype(jnp.bfloat16)
        act_all = lax.all_gather(act_blk, "tx", axis=0, tiled=True)
        mlp_out = lax.psum_scatter(jnp.dot(act_all, w_down_blk, preferred_element_type=jnp.float32),
                                   "ty", scatter_dimension=0, tiled=True)
        y_blk = (x_float + mlp_out).astype(jnp.bfloat16)

        dy_all = lax.all_gather(dy_blk, "ty", axis=0, tiled=True)
        dw_down_blk = contract_rows(act_all, dy_all)
        d_act = lax.psum_scatter(contract_cols(dy_all, w_down_blk), "tx", scatter_dimension=0, tiled=True)
        d_gate = (d_act * up_pre * gate_sig * (1.0 + gate_pre * (1.0 - gate_sig))).astype(jnp.bfloat16)
        d_up = (d_act * gate_swish).astype(jnp.bfloat16)
        d_gate_all = lax.all_gather(d_gate, "tx", axis=0, tiled=True)
        d_up_all = lax.all_gather(d_up, "tx", axis=0, tiled=True)
        dw_gate_blk = contract_rows(h_all, d_gate_all)
        dw_up_blk = contract_rows(h_all, d_up_all)
        d_hnorm = lax.psum_scatter(contract_cols(d_gate_all, w_gate_blk) + contract_cols(d_up_all, w_up_blk),
                                   "ty", scatter_dimension=0, tiled=True)
        value_a6 = d_hnorm * gain_blk
        bwd_stats = lax.psum(jnp.stack([jnp.sum(value_a6, axis=1), jnp.sum(value_a6 * x_hat, axis=1)]), "tx") / d_model
        dx_ln = inv_std * (value_a6 - bwd_stats[0][:, None] - x_hat * bwd_stats[1][:, None])
        dx_blk = (dy_blk.astype(jnp.float32) + dx_ln).astype(jnp.bfloat16)
        d_gain_blk = lax.psum(jnp.sum(d_hnorm * x_hat, axis=0), "ty")
        return (y_blk, dx_blk, dw_gate_blk, dw_up_blk, dw_down_blk, d_gain_blk)

    return jax.shard_map(
        local_step, mesh=mesh,
        in_specs=(P("ty", "tx"), P("ty", "tx"), P("tx"), P("tx", "ty"), P("tx", "ty"), P("ty", "tx")),
        out_specs=(P("ty", "tx"), P("ty", "tx"), P("tx", "ty"), P("tx", "ty"), P("ty", "tx"), P("tx")),
        check_vma=False)
```

profile of v0, /device:TPU:0, one launch (start us, length us, event | category | flops | bytes accessed | tf_op | source)
XLA Modules:
  0.0 398.5 jit_solution(8402334993202398899)
XLA Ops:
  7.2 0.0 reduce-scatter.12.cloned.1.call-start
  7.2 7.5 %all_gather.17 = bf16[256,512]{1,0:T(8,128)(2,1)S(1)} all-gather(bf16[128,512]{1,0:T(8,128)(2,1)} %param.7), channel_id=1, replica_groups=mesh['ty'=2,'tx'=8] {'ty'}, dimensions={0}, use_global_device_ids=true | all-gather | bytes 393216 | tf_op jit(solution)/shard_map/all_gather | solution.py:41
  14.7 9.2 %fusion.20 = f32[256,8192]{1,0:T(8,128)} fusion(bf16[256,512]{1,0:T(8,128)(2,1)S(1)} %all_gather.17, bf16[8192,512]{1,0:T(8,128)(2,1)} %param.11), kind=kOutput, calls=%fused_computation.38 | convolution fusion | flops 2147483648 | bytes 17039360 | tf_op jit(solution)/shard_map/dot_general | solution.py:14
  23.8 0.0 copy-start.2
  23.8 0.0 copy-start.4
  23.8 0.0 reduce-scatter.12.cloned.1.call-update
  23.9 0.0 reduce-scatter.8.cloned.1.call-start
  23.9 0.8 copy-done.2
  24.7 0.1 convert_reduce_fusion
  24.9 13.0 %psum.21 = f32[2,128]{1,0:T(2,128)S(1)} all-reduce(f32[2,128]{1,0:T(2,128)S(1)} %pad_maximum_fusion), channel_id=1, replica_groups=mesh['ty'=2,'tx'=8] {'tx'}, use_global_device_ids=true, to_apply=%region_2.0 | all-reduce | flops 256 | bytes 2048 | tf_op jit(solution)/shard_map/psum | solution.py:23
  37.9 0.0 copy-done.4
  37.9 0.1 fusion.7
  38.0 5.6 %all_gather.15 = bf16[256,512]{1,0:T(8,128)(2,1)S(1)} all-gather(bf16[128,512]{1,0:T(8,128)(2,1)S(1)} %fusion.7), channel_id=1, replica_groups=mesh['ty'=2,'tx'=8] {'ty'}, dimensions={0}, use_global_device_ids=true | all-gather | bytes 393216 | tf_op jit(solution)/shard_map/all_gather | solution.py:28
  43.6 9.1 %fusion.18 = f32[256,8192]{1,0:T(8,128)} fusion(bf16[256,512]{1,0:T(8,128)(2,1)S(1)} %all_gather.15, bf16[512,8192]{1,0:T(8,128)(2,1)} %param.10), kind=kOutput, calls=%fused_computation.36 | convolution fusion | flops 2147483648 | bytes 17039360 | tf_op jit(solution)/shard_map/dot_general | solution.py:31
  52.8 0.0 reduce-scatter.8.cloned.1.call-update
  52.8 0.0 reduce-scatter.6.cloned.1.call-start
  52.9 9.1 %fusion.17 = f32[256,8192]{1,0:T(8,128)} fusion(bf16[256,512]{1,0:T(8,128)(2,1)S(1)} %all_gather.15, bf16[512,8192]{1,0:T(8,128)(2,1)} %param.9), kind=kOutput, calls=%fused_computation.35 | convolution fusion | flops 2147483648 | bytes 17039360 | tf_op jit(solution)/shard_map/dot_general | solution.py:29
  62.0 0.0 reduce-scatter.6.cloned.1.call-update
  62.0 0.0 all-gather.6.cloned.1.call-start
  62.1 28.2 %reduce-scatter.12.cloned.1.call-done = f32[32,8192]{1,0:T(8,128)} async-done(((f32[256,8192]{1,0:T(8,128)}), f32[32,8192]{1,0:T(8,128)}) %reduce-scatter.12.cloned.1.call-update) | async-done | bytes 1048592 | tf_op jit(solution)/shard_map/reduce_scatter | solution.py:43
  90.2 69.0 %reduce-scatter.8.cloned.1.call-done = f32[32,8192]{1,0:T(8,128)} async-done(((f32[256,8192]{1,0:T(8,128)}), f32[32,8192]{1,0:T(8,128)}) %reduce-scatter.8.cloned.1.call-update) | async-done | bytes 1048592 | tf_op jit(solution)/shard_map/reduce_scatter | solution.py:31
  159.2 69.0 %reduce-scatter.6.cloned.1.call-done = f32[32,8192]{1,0:T(8,128)} async-done(((f32[256,8192]{1,0:T(8,128)}), f32[32,8192]{1,0:T(8,128)}) %reduce-scatter.6.cloned.1.call-update) | async-done | bytes 1048592 | tf_op jit(solution)/shard_map/reduce_scatter | solution.py:29
  228.3 3.4 multiply_convert_fusion
  231.7 0.0 all-gather.6.cloned.1.call-update
  231.7 0.0 all-gather.8.cloned.1.call-start
  231.8 0.5 all-gather.8.cloned.1.call-update
  232.3 0.0 all-gather.4.cloned.1.call-start
  232.4 0.5 all-gather.4.cloned.1.call-update
  232.9 0.2 reduce-scatter.14.cloned.1.call-start
  233.1 31.3 %all-gather.6.cloned.1.call-done = bf16[256,8192]{1,0:T(8,128)(2,1)} async-done(((bf16[32,8192]{1,0:T(8,128)(2,1)}), bf16[256,8192]{1,0:T(8,128)(2,1)}) %all-gather.6.cloned.1.call-update) | async-done | bytes 4194320 | tf_op jit(solution)/shard_map/all_gather | solution.py:46
  264.4 7.0 %fusion.21 = f32[256,512]{1,0:T(8,128)S(1)} fusion(bf16[256,8192]{1,0:T(8,128)(2,1)} %all-gather.6.cloned.1.call-done, bf16[512,8192]{1,0:T(8,128)(2,1)} %param.9), kind=kOutput, calls=%fused_computation.39 | convolution fusion | flops 2147483648 | bytes 13107200 | tf_op jit(solution)/shard_map/dot_general | solution.py:14
  271.5 27.8 %all-gather.8.cloned.1.call-done = bf16[256,8192]{1,0:T(8,128)(2,1)} async-done(((bf16[32,8192]{1,0:T(8,128)(2,1)}), bf16[256,8192]{1,0:T(8,128)(2,1)}) %all-gather.8.cloned.1.call-update) | async-done | bytes 4194320 | tf_op jit(solution)/shard_map/all_gather | solution.py:47
  299.3 7.8 %convolution_add_fusion = f32[256,512]{1,0:T(8,128)} fusion(f32[256,512]{1,0:T(8,128)S(1)} %fusion.21, bf16[256,8192]{1,0:T(8,128)(2,1)} %all-gather.8.cloned.1.call-done, bf16[512,8192]{1,0:T(8,128)(2,1)} %param.10), kind=kOutput, calls=%fused_computation | convolution fusion | flops 2147614720 | bytes 13631488 | tf_op jit(solution)/shard_map/dot_general | solution.py:14
  307.1 0.0 reduce-scatter.14.cloned.1.call-update
  307.2 0.3 reduce-scatter.10.cloned.1.call-start
  307.4 26.7 %all-gather.4.cloned.1.call-done = bf16[256,8192]{1,0:T(8,128)(2,1)} async-done(((bf16[32,8192]{1,0:T(8,128)(2,1)}), bf16[256,8192]{1,0:T(8,128)(2,1)}) %all-gather.4.cloned.1.call-update) | async-done | bytes 4194320 | tf_op jit(solution)/shard_map/all_gather | solution.py:36
  334.2 7.8 %fusion.19 = f32[256,512]{1,0:T(8,128)} fusion(bf16[256,8192]{1,0:T(8,128)(2,1)} %all-gather.4.cloned.1.call-done, bf16[8192,512]{1,0:T(8,128)(2,1)} %param.11), kind=kOutput, calls=%fused_computation.37 | convolution fusion | flops 2147483648 | bytes 13107200 | tf_op jit(solution)/shard_map/dot_general | solution.py:37
  342.0 0.0 reduce-scatter.10.cloned.1.call-update
  342.0 0.0 copy-start.1
  342.0 10.9 %fusion.24 = f32[8192,512]{1,0:T(8,128)} fusion(bf16[256,8192]{1,0:T(8,128)(2,1)} %all-gather.4.cloned.1.call-done, bf16[256,512]{1,0:T(8,128)(2,1)S(1)} %all_gather.17), kind=kOutput, calls=%fused_computation.42 | convolution fusion | flops 2147483648 | bytes 21233664 | tf_op jit(solution)/shard_map/dot_general | solution.py:10
  352.9 0.0 copy-done.1
  352.9 0.0 copy-start
  352.9 8.5 %fusion.23 = f32[512,8192]{1,0:T(8,128)} fusion(bf16[256,512]{1,0:T(8,128)(2,1)S(1)} %all_gather.15, bf16[256,8192]{1,0:T(8,128)(2,1)S(1)} %copy-done.1), kind=kOutput, calls=%fused_computation.41 | convolution fusion | flops 2147483648 | bytes 21233664 | tf_op jit(solution)/shard_map/dot_general | solution.py:10
  361.4 0.0 copy-done
  361.5 0.0 copy-start.3
  361.5 8.5 %fusion.22 = f32[512,8192]{1,0:T(8,128)} fusion(bf16[256,512]{1,0:T(8,128)(2,1)S(1)} %all_gather.15, bf16[256,8192]{1,0:T(8,128)(2,1)S(1)} %copy-done), kind=kOutput, calls=%fused_computation.40 | convolution fusion | flops 2147483648 | bytes 21233664 | tf_op jit(solution)/shard_map/dot_general | solution.py:10
  370.0 0.0 reduce-scatter.14.cloned.1.call-done
  370.0 1.2 fusion.13
  371.2 13.1 %psum.22 = f32[2,128]{1,0:T(2,128)S(1)} all-reduce(f32[2,128]{1,0:T(2,128)S(1)} %pad_maximum_fusion.1), channel_id=1, replica_groups=mesh['ty'=2,'tx'=8] {'tx'}, use_global_device_ids=true, to_apply=%region_10.0 | all-reduce | flops 256 | bytes 2048 | tf_op jit(solution)/shard_map/psum | solution.py:53
  384.3 5.5 %psum.23 = f32[512]{0:T(512)} all-reduce(f32[512]{0:T(512)S(1)} %get-tuple-element.6), channel_id=1, replica_groups=mesh['ty'=2,'tx'=8] {'ty'}, use_global_device_ids=true, to_apply=%region_12.0 | all-reduce | flops 512 | bytes 4096 | tf_op jit(solution)/shard_map/psum | solution.py:56
  389.8 0.0 reduce-scatter.10.cloned.1.call-done
  389.8 0.0 copy-done.3
  389.8 1.9 fusion.12
  (7 shorter events, 0.0 us)
Async XLA Ops:
  7.2 83.1 %reduce-scatter.12.cloned.1.call-start = ((), (), s32[]{:S(2)}) async-start(), calls=%async_computation.9 | async-start | bytes 9437184 | tf_op jit(solution)/shard_map/reduce_scatter | solution.py:43
  23.8 0.9 copy-start.2
  23.8 14.1 %copy-start.4 = (f32[512]{0:T(512)S(1)}, f32[512]{0:T(512)}, u32[]{:S(2)}) copy-start(f32[512]{0:T(512)} %param.8) | copy-start | bytes 6148
  23.9 135.4 %reduce-scatter.8.cloned.1.call-start = ((), (), s32[]{:S(2)}) async-start(), calls=%async_computation.6 | async-start | bytes 9437184 | tf_op jit(solution)/shard_map/reduce_scatter | solution.py:31
  52.8 175.5 %reduce-scatter.6.cloned.1.call-start = ((), (), s32[]{:S(2)}) async-start(), calls=%async_computation.5 | async-start | bytes 9437184 | tf_op jit(solution)/shard_map/reduce_scatter | solution.py:29
  62.0 202.4 %all-gather.6.cloned.1.call-start = ((), (), s32[]{:S(2)}) async-start(), calls=%async_computation.10 | async-start | bytes 4718592 | tf_op jit(solution)/shard_map/all_gather | solution.py:46
  231.7 67.6 %all-gather.8.cloned.1.call-start = ((), (), s32[]{:S(2)}) async-start(), calls=%async_computation.11 | async-start | bytes 4718592 | tf_op jit(solution)/shard_map/all_gather | solution.py:47
  232.3 101.8 %all-gather.4.cloned.1.call-start = ((), (), s32[]{:S(2)}) async-start(), calls=%async_computation.7 | async-start | bytes 4718592 | tf_op jit(solution)/shard_map/all_gather | solution.py:36
  232.9 137.1 %reduce-scatter.14.cloned.1.call-start = ((), (), s32[]{:S(2)}) async-start(), calls=%async_computation.12 | async-start | bytes 786432 | tf_op jit(solution)/shard_map/reduce_scatter | solution.py:50
  307.2 82.6 %reduce-scatter.10.cloned.1.call-start = ((), (), s32[]{:S(2)}) async-start(), calls=%async_computation.8 | async-start | bytes 786432 | tf_op jit(solution)/shard_map/reduce_scatter | solution.py:37
  342.0 10.9 %copy-start.1 = (bf16[256,8192]{1,0:T(8,128)(2,1)S(1)}, bf16[256,8192]{1,0:T(8,128)(2,1)}, u32[]{:S(2)}) copy-start(bf16[256,8192]{1,0:T(8,128)(2,1)} %all-gather.8.cloned.1.call-done) | copy-start | bytes 12582916
  352.9 8.5 %copy-start = (bf16[256,8192]{1,0:T(8,128)(2,1)S(1)}, bf16[256,8192]{1,0:T(8,128)(2,1)}, u32[]{:S(2)}) copy-start(bf16[256,8192]{1,0:T(8,128)(2,1)} %all-gather.6.cloned.1.call-done) | copy-start | bytes 12582916
  361.5 28.3 %copy-start.3 = (bf16[128,512]{1,0:T(8,128)(2,1)S(1)}, bf16[128,512]{1,0:T(8,128)(2,1)}, u32[]{:S(2)}) copy-start(bf16[128,512]{1,0:T(8,128)(2,1)} %param.7) | copy-start | bytes 393220
Sparse Core Ops, SparseCore 0:
  24.0 66.2 reduce-scatter.11
  94.2 64.9 reduce-scatter.7
  163.2 64.9 reduce-scatter.5
  231.8 32.5 all-gather.5
  266.7 32.5 all-gather.7
  301.6 32.5 all-gather.3
  336.4 12.6 reduce-scatter.13
  351.3 12.6 reduce-scatter.9
where the time goes:
time: 399 us; the launch traced here: 398 us
  waiting for transfers between devices  253 us (63%)
  matrix products  78.1 us (20%)
  blocking collectives  44.7 us (11%)
  between operations  14.2 us (4%)
  other arithmetic  6.7 us (2%)
    reduce_scatter x1, waiting for transfers between devices, local_step(): lax.psum_scatter(jnp.dot(h_all, w_gate_blk, preferred_element_type=jnp.fl...  69 us
    reduce_scatter x1, waiting for transfers between devices, local_step(): lax.psum_scatter(jnp.dot(h_all, w_up_blk, preferred_element_type=jnp.floa...  69 us
    all_gather x1, waiting for transfers between devices, local_step(): d_gate_all = lax.all_gather(d_gate, 'tx', axis=0, tiled=True)  31.3 us
    reduce_scatter x1, waiting for transfers between devices, local_step(): lax.psum_scatter(contract_cols(dy_all, w_down_blk), 'tx', scatter_dimensi...  28.2 us
    dot_general x3, matrix products, contract_rows(): lax.dot_general(left_op, right_op, (((0,), (0,)), ((), ())), preferred_el...  28 us
    all_gather x1, waiting for transfers between devices, local_step(): d_up_all = lax.all_gather(d_up, 'tx', axis=0, tiled=True)  27.8 us
    all_gather x1, waiting for transfers between devices, local_step(): act_all = lax.all_gather(act_blk, 'tx', axis=0, tiled=True)  26.7 us
    dot_general x3, matrix products, contract_cols(): lax.dot_general(left_op, right_op, (((1,), (1,)), ((), ())), preferred_el...  24 us
  transfers between devices with their start and end apart: 8, of which 6 were waited for; matrix products, arithmetic and copies ran while one was open for 18% of the time, Pallas kernels for 0%

commit v1 on v0

v1 whole, which is shorter than its diff:
```python
import functools

import jax
import jax.numpy as jnp
from jax import lax
from jax.experimental import pallas as pl
from jax.experimental.pallas import tpu as pltpu
from jax.sharding import PartitionSpec as P

LN_EPS = 1e-6
MESH = pl.DeviceIdType.MESH
FC = 512
P_SLOTS = 3
D_SLOTS = 4


def contract_rows(left_op, right_op):
    return lax.dot_general(left_op, right_op, (((0,), (0,)), ((), ())), preferred_element_type=jnp.float32)


def contract_cols(left_op, right_op):
    return lax.dot_general(left_op, right_op, (((1,), (1,)), ((), ())), preferred_element_type=jnp.float32)


def mo(value, multiple):
    return pl.multiple_of(value, multiple)


def branch_kernel(d_model, n_steps,
                  x_ref, dy_ref, gain_ref, wg_hbm, wu_hbm, wd_hbm,
                  a_hbm, du_hbm, dv_hbm, h_ref, dya_ref, m_own_ref, m_oth_ref, dh_own_ref, dh_oth_ref, dg_ref, cols_ref,
                  wg, wu, wd, xa, xh, part, dsum, r1, r2, gat, m_acc, dh_acc, st, sb, rb,
                  wsem, zs, zr, ss, sr, bs, br, ds, dr, p1s, p1r, p2s, p2r, g1s, g1r, g2s, g2r, gds, gdr, osem):
    half = FC // 2
    rows = x_ref.shape[0]
    tok = 2 * rows
    q1, q2, q3 = tok // 2, tok // 4, tok // 8

    ty = lax.axis_index("ty")
    t = lax.axis_index("tx")
    c = lax.rem(t, 2)
    xc = lax.rem(lax.div(t, 2), 2)
    yc = lax.div(t, 4)
    me = ty * 8 + t
    dev_c = (ty, t + 1 - 2 * c)
    dev_x = (ty, t + 2 - 4 * xc)
    dev_y = (ty, t + 4 - 8 * yc)
    dev_z = (1 - ty, t)

    def remote(src, dst, ssem, rsem, dev):
        return pltpu.make_async_remote_copy(src_ref=src, dst_ref=dst, send_sem=ssem, recv_sem=rsem,
                                            device_id=dev, device_id_type=MESH)

    def wcopy(k, i):
        cs = pl.ds(mo(i * FC, FC), FC)
        if k == 0:
            return pltpu.make_async_copy(wg_hbm.at[:, cs], wg.at[:, cs], wsem.at[0, i])
        if k == 1:
            return pltpu.make_async_copy(wu_hbm.at[:, cs], wu.at[:, cs], wsem.at[1, i])
        return pltpu.make_async_copy(wd_hbm.at[cs, :], wd.at[cs, :], wsem.at[2, i])

    def start_w(i, carry):
        for k in range(3):
            wcopy(k, i).start()
        return carry

    lax.fori_loop(0, n_steps, start_w, 0)

    barrier = pltpu.get_barrier_semaphore()
    for o in range(1, 16):
        q = lax.rem(me + o, 16)
        pl.semaphore_signal(barrier, inc=1, device_id=(lax.div(q, 8), lax.rem(q, 8)), device_id_type=MESH)
    pl.semaphore_wait(barrier, 15)

    own = pl.ds(mo(ty * rows, rows), rows)
    oth = pl.ds(mo((1 - ty) * rows, rows), rows)

    zx = remote(x_ref, xa.at[own, :], zs.at[0], zr.at[0], dev_z)
    zx.start()
    zdy = remote(dy_ref, dya_ref.at[own, :], zs.at[1], zr.at[1], dev_z)
    zdy.start()

    lane = lax.broadcasted_iota(jnp.int32, (rows, 128), 1)

    def pack_cols(c0, c1):
        both = jnp.where(lane == 0, c0, jnp.where(lane == 1, c1, 0.0))
        return both.T[0:8, :]

    def unpack_cols(packed):
        full = jnp.concatenate([packed, jnp.zeros((rows - 8, 128), jnp.float32)], axis=0).T
        return full[:, 0:1], full[:, 1:2]

    x_own = x_ref[...].astype(jnp.float32)
    st[me] = pack_cols(jnp.sum(x_own, axis=1, keepdims=True), jnp.sum(x_own * x_own, axis=1, keepdims=True))
    for o in range(1, 16):
        q = lax.rem(me + o, 16)
        remote(st.at[me], st.at[me], ss.at[o], sr.at[o], (lax.div(q, 8), lax.rem(q, 8))).start()

    xa[own, :] = x_ref[...]
    dya_ref[own, :] = dy_ref[...]
    for o in range(1, 16):
        q = lax.rem(me + 16 - o, 16)
        d = remote(st.at[me], st.at[q], ss.at[o], sr.at[o], (lax.div(q, 8), lax.rem(q, 8)))
        d.wait_send()
        d.wait_recv()
    zx.wait_send()
    remote(x_ref, xa.at[oth, :], zs.at[0], zr.at[0], dev_z).wait_recv()

    gain = gain_ref[...]
    stat_cols = []
    for k in range(2):
        s = st[8 * k]
        for j in range(1, 8):
            s = s + st[8 * k + j]
        c0, c1 = unpack_cols(s)
        mean = c0 / d_model
        inv = lax.rsqrt(c1 / d_model - mean * mean + LN_EPS)
        rs = slice(k * rows, (k + 1) * rows)
        xhat = (xa[rs, :].astype(jnp.float32) - mean) * inv
        xh[rs, :] = xhat
        h_ref[rs, :] = (gain * xhat).astype(jnp.bfloat16)
        stat_cols.append((mean, inv))
    mean_own = jnp.where(ty == 0, stat_cols[0][0], stat_cols[1][0])
    inv_own = jnp.where(ty == 0, stat_cols[0][1], stat_cols[1][1])
    cols_ref[...] = jnp.where(lane == 0, mean_own, jnp.where(lane == 1, inv_own, 0.0))

    m_acc[...] = jnp.zeros_like(m_acc)
    dh_acc[...] = jnp.zeros_like(dh_acc)
    zdy.wait_send()
    remote(dy_ref, dya_ref.at[oth, :], zs.at[1], zr.at[1], dev_z).wait_recv()

    ca = slice(0, half)
    cb = slice(half, FC)

    def seg(base, size, mult):
        return pl.ds(mo(base, mult), size)

    own_c = seg(c * q1, q1, q1)
    oth_c = seg((1 - c) * q1, q1, q1)
    a_keep = seg(c * q1 + xc * q2, q2, q2)
    a_send = seg(c * q1 + (1 - xc) * q2, q2, q2)
    b_keep = seg(c * q1 + yc * q2, q2, q2)
    b_send = seg(c * q1 + (1 - yc) * q2, q2, q2)
    a_fin = seg(c * q1 + xc * q2 + yc * q3, q3, q3)
    a_fin_n = seg(c * q1 + xc * q2 + (1 - yc) * q3, q3, q3)
    b_fin = seg(c * q1 + yc * q2 + xc * q3, q3, q3)
    b_fin_n = seg(c * q1 + yc * q2 + (1 - xc) * q3, q3, q3)
    r_keep = (seg(yc * q3, q3, q3), seg(xc * q3, q3, q3))
    r_send = (seg((1 - yc) * q3, q3, q3), seg((1 - xc) * q3, q3, q3))
    keep1, send1 = (a_keep, b_keep), (a_send, b_send)
    fin, fin_n = (a_fin, b_fin), (a_fin_n, b_fin_n)
    colw = (ca, cb)
    dev1, dev2 = (dev_x, dev_y), (dev_y, dev_x)

    def gcols(j, r):
        return pl.ds(mo(j * FC + r * half, half), half)

    def d_copy(j):
        return remote(part.at[lax.rem(j, P_SLOTS), :, oth_c, :], dsum.at[lax.rem(j, D_SLOTS)], ds.at[j], dr.at[j], dev_c)

    def p1_copy(j, r):
        return remote(part.at[lax.rem(j, P_SLOTS), :, send1[r], colw[r]], r1.at[j, r], p1s.at[r, j], p1r.at[r, j], dev1[r])

    def p2_copy(j, r):
        return remote(r1.at[j, r, :, r_send[r], :], r2.at[j, r], p2s.at[r, j], p2r.at[r, j], dev2[r])

    def g1_copy(j, r):
        ref = gat.at[:, fin[r], gcols(j, r)]
        return remote(ref, ref, g1s.at[r, j], g1r.at[r, j], dev2[r])

    def g1_in(j, r):
        ref = gat.at[:, fin_n[r], gcols(j, r)]
        return remote(ref, ref, g1s.at[r, j], g1r.at[r, j], dev2[r])

    def g2_copy(j, r):
        ref = gat.at[:, keep1[r], gcols(j, r)]
        return remote(ref, ref, g2s.at[r, j], g2r.at[r, j], dev1[r])

    def g2_in(j, r):
        ref = gat.at[:, send1[r], gcols(j, r)]
        return remote(ref, ref, g2s.at[r, j], g2r.at[r, j], dev1[r])

    def gd_copy(j, side):
        ref = gat.at[:, side, pl.ds(mo(j * FC, FC), FC)]
        return remote(ref, ref, gds.at[j], gdr.at[j], dev_c)

    def out_copy(j, k):
        cs = pl.ds(mo(j * FC, FC), FC)
        dst = (a_hbm, du_hbm, dv_hbm)[k]
        return pltpu.make_async_copy(gat.at[k, :, cs], dst.at[:, cs], osem.at[k, j])

    def step(i, carry):
        @pl.when(jnp.logical_and(i >= P_SLOTS, i < n_steps + P_SLOTS))
        def _():
            j = i - P_SLOTS
            d_copy(j).wait_send()
            for r in range(2):
                p1_copy(j, r).wait_send()

        @pl.when(i < n_steps)
        def _():
            for k in range(3):
                wcopy(k, i).wait()
            cs = pl.ds(mo(i * FC, FC), FC)
            slot = lax.rem(i, P_SLOTS)
            h = h_ref[...]
            part[slot, 0] = jnp.dot(h, wg[:, cs], preferred_element_type=jnp.float32)
            part[slot, 1] = jnp.dot(h, wu[:, cs], preferred_element_type=jnp.float32)
            part[slot, 2] = contract_cols(dya_ref[...], wd[cs, :])
            d_copy(i).start()

        @pl.when(jnp.logical_and(i >= 1, i < n_steps + 1))
        def _():
            j = i - 1
            d_copy(j).wait_recv()
            slot = lax.rem(j, P_SLOTS)
            dslot = lax.rem(j, D_SLOTS)
            for k in range(3):
                part[slot, k, own_c, :] = part[slot, k, own_c, :] + dsum[dslot, k]
            for r in range(2):
                p1_copy(j, r).start()

        @pl.when(jnp.logical_and(i >= 2, i < n_steps + 2))
        def _():
            j = i - 2
            slot = lax.rem(j, P_SLOTS)
            for r in range(2):
                p1_copy(j, r).wait_recv()
                for k in range(3):
                    r1[j, r, k] = r1[j, r, k] + part[slot, k, keep1[r], colw[r]]
                p2_copy(j, r).start()

        @pl.when(jnp.logical_and(i >= 3, i < n_steps + 3))
        def _():
            j = i - 3
            for r in range(2):
                p2_copy(j, r).wait_recv()
                u = r1[j, r, 0, r_keep[r], :] + r2[j, r, 0]
                v = r1[j, r, 1, r_keep[r], :] + r2[j, r, 1]
                da = r1[j, r, 2, r_keep[r], :] + r2[j, r, 2]
                sig = jax.nn.sigmoid(u)
                swish = u * sig
                cs = gcols(j, r)
                gat[0, fin[r], cs] = (swish * v).astype(jnp.bfloat16)
                gat[1, fin[r], cs] = (da * v * sig * (1.0 + u * (1.0 - sig))).astype(jnp.bfloat16)
                gat[2, fin[r], cs] = (da * swish).astype(jnp.bfloat16)
                g1_copy(j, r).start()

        @pl.when(jnp.logical_and(i >= 4, i < n_steps + 4))
        def _():
            j = i - 4
            for r in range(2):
                g1_in(j, r).wait_recv()
                g2_copy(j, r).start()

        @pl.when(jnp.logical_and(i >= 5, i < n_steps + 5))
        def _():
            j = i - 5
            for r in range(2):
                g2_in(j, r).wait_recv()
            gd_copy(j, own_c).start()

        @pl.when(i >= 6)
        def _():
            j = i - 6
            gd_copy(j, oth_c).wait_recv()
            for k in range(3):
                out_copy(j, k).start()
            cs = pl.ds(mo(j * FC, FC), FC)
            m_acc[...] += jnp.dot(gat[0, :, cs], wd[cs, :], preferred_element_type=jnp.float32)
            dh_acc[...] += contract_cols(gat[1, :, cs], wg[:, cs]) + contract_cols(gat[2, :, cs], wu[:, cs])
            for r in range(2):
                p2_copy(j, r).wait_send()
                g1_copy(j, r).wait_send()
                g2_copy(j, r).wait_send()
            gd_copy(j, own_c).wait_send()
        return carry

    lax.fori_loop(0, n_steps + 6, step, 0)

    for k in range(2):
        rs = slice(k * rows, (k + 1) * rows)
        e = dh_acc[rs, :] * gain
        sb[k] = pack_cols(jnp.sum(e, axis=1, keepdims=True), jnp.sum(e * xh[rs, :], axis=1, keepdims=True))
    rb[me] = sb[ty]
    for o in range(1, 16):
        q = lax.rem(me + o, 16)
        remote(sb.at[lax.div(q, 8)], rb.at[me], bs.at[o], br.at[o], (lax.div(q, 8), lax.rem(q, 8))).start()
    dg_ref[...] = jnp.sum(dh_acc[...] * xh[...], axis=0, keepdims=True)
    m_own_ref[...] = m_acc[own, :]
    m_oth_ref[...] = m_acc[oth, :]
    dh_own_ref[...] = dh_acc[own, :]
    dh_oth_ref[...] = dh_acc[oth, :]
    for o in range(1, 16):
        q = lax.rem(me + 16 - o, 16)
        d = remote(sb.at[0], rb.at[q], bs.at[o], br.at[o], (lax.div(q, 8), lax.rem(q, 8)))
        d.wait_send()
        d.wait_recv()
    s = rb[0]
    for j in range(1, 16):
        s = s + rb[j]
    c0, c1 = unpack_cols(s)
    cols_ref[...] = jnp.where(lane == 2, c0 / d_model, jnp.where(lane == 3, c1 / d_model, cols_ref[...]))

    def drain(j, carry):
        for k in range(3):
            out_copy(j, k).wait()
        return carry

    lax.fori_loop(0, n_steps, drain, 0)


def solution(mesh):
    tx_size = mesh.shape["tx"]
    ty_size = mesh.shape["ty"]

    def local_step(x_blk, dy_blk, gain_blk, w_gate_blk, w_up_blk, w_down_blk):
        rows, dl = x_blk.shape
        fl = w_gate_blk.shape[1]
        tok = rows * ty_size
        d_model = dl * tx_size
        n = fl // FC
        half = FC // 2
        f32, bf16 = jnp.float32, jnp.bfloat16
        vm = pl.BlockSpec(memory_space=pltpu.VMEM)
        anyspec = pl.BlockSpec(memory_space=pl.ANY)
        sem = pltpu.SemaphoreType.DMA
        S = jax.ShapeDtypeStruct
        outs = pl.pallas_call(
            functools.partial(branch_kernel, d_model, n),
            out_shape=[S((tok, fl), bf16)] * 3 + [S((tok, dl), bf16)] * 2 + [S((rows, dl), f32)] * 4
            + [S((1, dl), f32), S((rows, 128), f32)],
            in_specs=[vm] * 3 + [anyspec] * 3,
            out_specs=[anyspec] * 3 + [vm] * 8,
            scratch_shapes=[
                pltpu.VMEM((dl, fl), bf16), pltpu.VMEM((dl, fl), bf16), pltpu.VMEM((fl, dl), bf16),
                pltpu.VMEM((tok, dl), bf16), pltpu.VMEM((tok, dl), f32),
                pltpu.VMEM((P_SLOTS, 3, tok, FC), f32),
                pltpu.VMEM((D_SLOTS, 3, tok // 2, FC), f32),
                pltpu.VMEM((n, 2, 3, tok // 4, half), f32),
                pltpu.VMEM((n, 2, 3, tok // 8, half), f32),
                pltpu.VMEM((3, tok, fl), bf16),
                pltpu.VMEM((tok, dl), f32), pltpu.VMEM((tok, dl), f32),
                pltpu.VMEM((16, 8, 128), f32), pltpu.VMEM((2, 8, 128), f32), pltpu.VMEM((16, 8, 128), f32),
                sem((3, n)), sem((2,)), sem((2,)), sem((16,)), sem((16,)), sem((16,)), sem((16,)),
                sem((n,)), sem((n,)), sem((2, n)), sem((2, n)), sem((2, n)), sem((2, n)),
                sem((2, n)), sem((2, n)), sem((2, n)), sem((2, n)), sem((n,)), sem((n,)), sem((3, n)),
            ],
            compiler_params=pltpu.CompilerParams(collective_id=0, has_side_effects=True, vmem_limit_bytes=62 * 1024 * 1024),
            cost_estimate=pl.CostEstimate(flops=12 * tok * dl * fl, bytes_accessed=6 * dl * fl + 6 * tok * fl, transcendentals=0),
        )(x_blk, dy_blk, gain_blk[None, :], w_gate_blk, w_up_blk, w_down_blk)
        (a_all, du_all, dv_all, h_all, dy_all, m_own, m_oth, dh_own, dh_oth, dg, cols) = outs

        swap = [(0, 1), (1, 0)]
        m_in = lax.ppermute(m_oth, "ty", swap)
        dh_in = lax.ppermute(dh_oth, "ty", swap)
        dg_in = lax.ppermute(dg, "ty", swap)
        dw_gate_blk = contract_rows(h_all, du_all)
        dw_up_blk = contract_rows(h_all, dv_all)
        dw_down_blk = contract_rows(a_all, dy_all)

        x_float = x_blk.astype(f32)
        y_blk = (x_float + (m_own + m_in)).astype(bf16)
        mean_x, inv_std, mean_e, mean_ex = cols[:, 0:1], cols[:, 1:2], cols[:, 2:3], cols[:, 3:4]
        x_hat = (x_float - mean_x) * inv_std
        e = (dh_own + dh_in) * gain_blk
        dx_ln = inv_std * (e - mean_e - x_hat * mean_ex)
        dx_blk = (dy_blk.astype(f32) + dx_ln).astype(bf16)
        d_gain_blk = (dg + dg_in)[0]
        return (y_blk, dx_blk, dw_gate_blk, dw_up_blk, dw_down_blk, d_gain_blk)

    return jax.shard_map(
        local_step, mesh=mesh,
        in_specs=(P("ty", "tx"), P("ty", "tx"), P("tx"), P("tx", "ty"), P("tx", "ty"), P("ty", "tx")),
        out_specs=(P("ty", "tx"), P("ty", "tx"), P("tx", "ty"), P("tx", "ty"), P("ty", "tx"), P("tx")),
        check_vma=False)
```

time: 399 us -> 216 us (0.54)
  waiting for transfers between devices: 253 us -> 0.01 us
  Pallas kernels: 0 us -> 182 us
  matrix products: 78.1 us -> 28 us
  blocking collectives: 44.7 us -> 0 us
  between operations: 14.2 us -> 0.76 us
  other arithmetic: 6.7 us -> 1.41 us
    pallas_call x0 -> x1, Pallas kernels: none -> 182 us  [local_step(): pl.pallas_call(functools.partial(branch_kernel, d_model, n), out_shape=[S...]
    reduce_scatter x5 -> x0, waiting for transfers between devices: 166 us -> none  [the longest x1 69 us: local_step(): lax.psum_scatter(jnp.dot(h_all, w_gate_blk, preferred_element_type=jnp.fl...]
    all_gather x3 -> x0, waiting for transfers between devices: 85.9 us -> none  [the longest x1 31.3 us: local_step(): d_gate_all = lax.all_gather(d_gate, 'tx', axis=0, tiled=True)]
    dot_general x6 -> x0, matrix products: 50.1 us -> none  [the longest x3 24 us: contract_cols(): lax.dot_general(left_op, right_op, (((1,), (1,)), ((), ())), preferred_el...]
    psum x3 -> x0, blocking collectives: 31.6 us -> none  [the longest x1 13.1 us: local_step(): lax.psum(jnp.stack([jnp.sum(value_a6, axis=1), jnp.sum(value_a6 * x_hat,...]
    all_gather x2 -> x0, blocking collectives: 13.1 us -> none  [the longest x1 7.46 us: local_step(): dy_all = lax.all_gather(dy_blk, 'ty', axis=0, tiled=True)]
    convert_element_type x3 -> x1, other arithmetic: 5.39 us -> 0.83 us  [local_step(): dx_blk = (dy_blk.astype(f32) + dx_ln).astype(bf16)]
  transfers between devices with their start and end apart: 8 -> 3, of which waited for: 6 -> 0; matrix products, arithmetic and copies ran while one was open for 18% -> 13% of each run, Pallas kernels for 0% -> 0%
where the time goes in v1:
time: 216 us
  Pallas kernels  182 us (84%)
  matrix products  28 us (13%)
  starting transfers between devices  2.83 us (1%)
    pallas_call x1, Pallas kernels, local_step(): pl.pallas_call(functools.partial(branch_kernel, d_model, n), out_shape=[S...  182 us
    dot_general x3, matrix products, contract_rows(): lax.dot_general(left_op, right_op, (((0,), (0,)), ((), ())), preferred_el...  28 us
  transfers between devices with their start and end apart: 3, of which 0 were waited for; matrix products, arithmetic and copies ran while one was open for 13% of the time, Pallas kernels for 0%

profile of v1, /device:TPU:0, one launch (start us, length us, event | category | flops | bytes accessed | tf_op | source)
XLA Modules:
  0.0 215.7 jit_solution(18424702215088687492)
XLA Ops:
  0.6 182.4 %shard_map.109 = (bf16[256,8192]{1,0:T(8,128)(2,1)}, bf16[256,8192]{1,0:T(8,128)(2,1)}, bf16[256,8192]{1,0:T(8,128)(2,1)}, bf16[256,512]{1,0:T(8,128)(2,1)}, bf1...) custom-call(bf16[128,512]{1,0:T(8,128)(2,1)} %x_ref.1, ...), custom_call_target="tpu_custom_call" | custom-call | flops 12884901888 | bytes 37748736 | tf_op jit(solution)/shard_map/pallas_call | solution.py:329
  183.0 0.8 collective-permute-start.2
  183.8 1.3 collective-permute-start
  185.1 0.8 collective-permute-start.1
  185.9 0.0 copy-start.1
  185.9 0.0 copy-start.6
  185.9 11.0 %fusion.7 = f32[512,8192]{1,0:T(8,128)} fusion(bf16[256,512]{1,0:T(8,128)(2,1)} %get-tuple-element.22, bf16[256,8192]{1,0:T(8,128)(2,1)} %get-tuple-element.23), kind=kOutput, calls=%fused_computation.13 | convolution fusion | flops 2147483648 | bytes 21233664 | tf_op jit(solution)/shard_map/dot_general | solution.py:18
  196.8 0.0 copy-done.1
  196.8 0.0 copy-done.6
  196.8 0.0 copy-start
  196.8 0.0 copy-start.3
  196.8 8.5 %fusion.9 = f32[8192,512]{1,0:T(8,128)} fusion(bf16[256,8192]{1,0:T(8,128)(2,1)S(1)} %copy-done.1, bf16[256,512]{1,0:T(8,128)(2,1)S(1)} %copy-done.6), kind=kOutput, calls=%fused_computation.15 | convolution fusion | flops 2147483648 | bytes 21233664 | tf_op jit(solution)/shard_map/dot_general | solution.py:18
  205.4 0.0 copy-done
  205.4 0.0 copy-done.3
  205.4 0.0 copy-start.2
  205.4 0.0 copy-start.10
  205.4 0.0 copy-start.4
  205.4 0.0 copy-start.5
  205.4 0.0 copy-start.7
  205.4 0.0 copy-start.8
  205.4 0.0 copy-start.9
  205.4 8.5 %fusion.8 = f32[512,8192]{1,0:T(8,128)} fusion(bf16[256,512]{1,0:T(8,128)(2,1)S(1)} %copy-done.3, bf16[256,8192]{1,0:T(8,128)(2,1)S(1)} %copy-done), kind=kOutput, calls=%fused_computation.14 | convolution fusion | flops 2147483648 | bytes 21233664 | tf_op jit(solution)/shard_map/dot_general | solution.py:18
  214.0 0.0 copy-done.2
  214.0 0.2 slice_reduce_fusion.3
  214.2 0.0 collective-permute-done.2
  214.2 0.0 copy-done.10
  214.2 0.6 add.19
  214.8 0.0 collective-permute-done
  214.8 0.0 collective-permute-done.1
  214.8 0.0 copy-done.4
  214.8 0.0 copy-done.5
  214.8 0.0 copy-done.7
  214.9 0.0 copy-done.8
  214.9 0.0 copy-done.9
  214.9 0.8 fusion.6
Async XLA Ops:
  183.0 31.2 %collective-permute-start.2 = (f32[1,512]{1,0:T(1,128)}, f32[1,512]{1,0:T(1,128)S(1)}, u32[]{:S(2)}, u32[]{:S(2)}) collective-permute-start(f32[1,512]{1,0:T(1,128)} %get-tuple-element.27), channel_id=1, source_target_pairs={{0,8},{8,0},{1,9},{9,1},{2,10},{10,2},{3,11},{11,3},{4,12},{12,4},... | collective-permute-start | bytes 6152 | tf_op jit(solution)/shard_map/ppermute | solution.py:357
  183.8 31.0 %collective-permute-start = (f32[128,512]{1,0:T(8,128)}, f32[128,512]{1,0:T(8,128)S(1)}, u32[]{:S(2)}, u32[]{:S(2)}) collective-permute-start(f32[128,512]{1,0:T(8,128)} %get-tuple-element.18), channel_id=1, source_target_pairs={{0,8},{8,0},{1,9},{9,1},{2,10},{10,2},{3,11},{11,3},{4,12},{12,4},... | collective-permute-start | bytes 786440 | tf_op jit(solution)/shard_map/ppermute | solution.py:355
  185.1 29.7 %collective-permute-start.1 = (f32[128,512]{1,0:T(8,128)}, f32[128,512]{1,0:T(8,128)S(1)}, u32[]{:S(2)}, u32[]{:S(2)}) collective-permute-start(f32[128,512]{1,0:T(8,128)} %get-tuple-element.21), channel_id=1, source_target_pairs={{0,8},{8,0},{1,9},{9,1},{2,10},{10,2},{3,11},{11,3},{4,12},{12,4},... | collective-permute-start | bytes 786440 | tf_op jit(solution)/shard_map/ppermute | solution.py:356
  185.9 11.0 %copy-start.1 = (bf16[256,8192]{1,0:T(8,128)(2,1)S(1)}, bf16[256,8192]{1,0:T(8,128)(2,1)}, u32[]{:S(2)}) copy-start(bf16[256,8192]{1,0:T(8,128)(2,1)} %get-tuple-element.25) | copy-start | bytes 12582916
  185.9 11.0 %copy-start.6 = (bf16[256,512]{1,0:T(8,128)(2,1)S(1)}, bf16[256,512]{1,0:T(8,128)(2,1)}, u32[]{:S(2)}) copy-start(bf16[256,512]{1,0:T(8,128)(2,1)} %get-tuple-element.26) | copy-start | bytes 786436
  196.8 8.6 %copy-start = (bf16[256,8192]{1,0:T(8,128)(2,1)S(1)}, bf16[256,8192]{1,0:T(8,128)(2,1)}, u32[]{:S(2)}) copy-start(bf16[256,8192]{1,0:T(8,128)(2,1)} %get-tuple-element.24) | copy-start | bytes 12582916
  196.8 8.6 %copy-start.3 = (bf16[256,512]{1,0:T(8,128)(2,1)S(1)}, bf16[256,512]{1,0:T(8,128)(2,1)}, u32[]{:S(2)}) copy-start(bf16[256,512]{1,0:T(8,128)(2,1)} %get-tuple-element.22) | copy-start | bytes 786436
  205.4 8.6 %copy-start.2 = (f32[128,128]{1,0:T(8,128)S(1)}, f32[128,128]{1,0:T(8,128)}, u32[]{:S(2)}) copy-start(f32[128,128]{1,0:T(8,128)} %get-tuple-element.19) | copy-start | bytes 196612
  205.4 8.8 %copy-start.10 = (f32[1,512]{1,0:T(1,128)S(1)}, f32[1,512]{1,0:T(1,128)}, u32[]{:S(2)}) copy-start(f32[1,512]{1,0:T(1,128)} %get-tuple-element.27) | copy-start | bytes 6148
  205.4 9.4 %copy-start.4 = (f32[128,512]{1,0:T(8,128)S(1)}, f32[128,512]{1,0:T(8,128)}, u32[]{:S(2)}) copy-start(f32[128,512]{1,0:T(8,128)} %get-tuple-element.17) | copy-start | bytes 786436
  205.4 9.4 %copy-start.5 = (f32[128,512]{1,0:T(8,128)S(1)}, f32[128,512]{1,0:T(8,128)}, u32[]{:S(2)}) copy-start(f32[128,512]{1,0:T(8,128)} %get-tuple-element.20) | copy-start | bytes 786436
  205.4 9.4 %copy-start.7 = (bf16[128,512]{1,0:T(8,128)(2,1)S(1)}, bf16[128,512]{1,0:T(8,128)(2,1)}, u32[]{:S(2)}) copy-start(bf16[128,512]{1,0:T(8,128)(2,1)} %x_ref.1) | copy-start | bytes 393220
  205.4 9.4 %copy-start.8 = (bf16[128,512]{1,0:T(8,128)(2,1)S(1)}, bf16[128,512]{1,0:T(8,128)(2,1)}, u32[]{:S(2)}) copy-start(bf16[128,512]{1,0:T(8,128)(2,1)} %dy_ref.1) | copy-start | bytes 393220
  205.4 9.4 %copy-start.9 = (f32[512]{0:T(512)S(1)}, f32[512]{0:T(512)}, u32[]{:S(2)}) copy-start(f32[512]{0:T(512)} %param.8) | copy-start | bytes 6148

commit v2 on v1

v2 whole, which is shorter than its diff:
```python
import functools

import jax
import jax.numpy as jnp
from jax import lax
from jax.experimental import pallas as pl
from jax.experimental.pallas import tpu as pltpu
from jax.sharding import PartitionSpec as P

LN_EPS = 1e-6
MESH = pl.DeviceIdType.MESH
FC = 512
OWN_FIRST = 2
P_SLOTS = 4
D_SLOTS = 4
RING = 8


def contract_rows(left_op, right_op):
    return lax.dot_general(left_op, right_op, (((0,), (0,)), ((), ())), preferred_element_type=jnp.float32)


def contract_cols(left_op, right_op):
    return lax.dot_general(left_op, right_op, (((1,), (1,)), ((), ())), preferred_element_type=jnp.float32)


def mo(value, multiple):
    return pl.multiple_of(value, multiple)


def branch_kernel(d_model, n_f,
                  x_ref, dy_ref, gain_ref, wg_hbm, wu_hbm, wd_hbm,
                  a_hbm, du_hbm, dv_hbm, h_ref, dya_ref, y_ref, dx_ref, dg_ref,
                  wg, wu, wd, xh, part, dsum, r1, r2, gat, acc, zin, st, rb, dgs, dgr,
                  wsem, zs, zr, ss, sr, bs, br, ds, dr, p1s, p1r, p2s, p2r, g1s, g1r, g2s, g2r, gds, gdr, osem):
    half = FC // 2
    rows = x_ref.shape[0]
    q1, q2, q3 = rows // 2, rows // 4, rows // 8
    n_units = 2 * n_f
    last_oth = OWN_FIRST + n_f - 1

    ty = lax.axis_index("ty")
    t = lax.axis_index("tx")
    c = lax.rem(t, 2)
    xc = lax.rem(lax.div(t, 2), 2)
    yc = lax.div(t, 4)
    dev_c = (ty, t + 1 - 2 * c)
    dev_x = (ty, t + 2 - 4 * xc)
    dev_y = (ty, t + 4 - 8 * yc)
    dev_z = (1 - ty, t)

    def remote(src, dst, ssem, rsem, dev):
        return pltpu.make_async_remote_copy(src_ref=src, dst_ref=dst, send_sem=ssem, recv_sem=rsem,
                                            device_id=dev, device_id_type=MESH)

    def f_of(j):
        return lax.rem(j + (n_f - OWN_FIRST), n_f)

    def oth_of(j):
        return lax.rem(lax.div(j + (n_f - OWN_FIRST), n_f), 2)

    def base_of(j):
        k = oth_of(j)
        return (ty + k - 2 * ty * k) * rows

    def fcols(j):
        return pl.ds(mo(f_of(j) * FC, FC), FC)

    def trows(j):
        return pl.ds(mo(base_of(j), rows), rows)

    def wcopy(k, i):
        cs = fcols(i)
        if k == 0:
            return pltpu.make_async_copy(wg_hbm.at[:, cs], wg.at[:, cs], wsem.at[0, i])
        if k == 1:
            return pltpu.make_async_copy(wu_hbm.at[:, cs], wu.at[:, cs], wsem.at[1, i])
        return pltpu.make_async_copy(wd_hbm.at[cs, :], wd.at[cs, :], wsem.at[2, i])

    def start_w(i, carry):
        for k in range(3):
            wcopy(k, i).start()
        return carry

    lax.fori_loop(0, n_f, start_w, 0)

    barrier = pltpu.get_barrier_semaphore()
    for o in range(1, 8):
        pl.semaphore_signal(barrier, inc=1, device_id=(ty, lax.rem(t + o, 8)), device_id_type=MESH)
    pl.semaphore_signal(barrier, inc=1, device_id=dev_z, device_id_type=MESH)

    own = pl.ds(mo(ty * rows, rows), rows)
    oth = pl.ds(mo((1 - ty) * rows, rows), rows)
    lane = lax.broadcasted_iota(jnp.int32, (rows, 128), 1)

    def pack_cols(c0, c1):
        both = jnp.where(lane == 0, c0, jnp.where(lane == 1, c1, 0.0))
        return both.T[0:8, :]

    def unpack_cols(packed):
        full = jnp.concatenate([packed, jnp.zeros((rows - 8, 128), jnp.float32)], axis=0).T
        return full[:, 0:1], full[:, 1:2]

    def send_stats(buf, ssem, rsem):
        for o in range(1, 8):
            remote(buf.at[t], buf.at[t], ssem.at[o], rsem.at[o], (ty, lax.rem(t + o, 8))).start()

    def total_stats(buf, ssem, rsem):
        for o in range(1, 8):
            q = lax.rem(t + 8 - o, 8)
            d = remote(buf.at[t], buf.at[q], ssem.at[o], rsem.at[o], (ty, q))
            d.wait_send()
            d.wait_recv()
        s = buf[0]
        for j in range(1, 8):
            s = s + buf[j]
        return unpack_cols(s)

    x_own = x_ref[...].astype(jnp.float32)
    st[t] = pack_cols(jnp.sum(x_own, axis=1, keepdims=True), jnp.sum(x_own * x_own, axis=1, keepdims=True))
    pl.semaphore_wait(barrier, 8)
    send_stats(st, ss, sr)
    zdy = remote(dy_ref, dya_ref.at[own, :], zs.at[0], zr.at[0], dev_z)
    zdy.start()
    dya_ref[own, :] = dy_ref[...]
    acc[...] = jnp.zeros_like(acc)

    gain = gain_ref[...]
    c0, c1 = total_stats(st, ss, sr)
    mean_x = c0 / d_model
    inv_std = lax.rsqrt(c1 / d_model - mean_x * mean_x + LN_EPS)
    xhat = (x_ref[...].astype(jnp.float32) - mean_x) * inv_std
    xh[...] = xhat
    h_ref[own, :] = (gain * xhat).astype(jnp.bfloat16)

    def h_copy(block):
        return remote(h_ref.at[own, :], h_ref.at[block, :], zs.at[1], zr.at[1], dev_z)

    h_copy(own).start()

    def seg(base, size):
        return pl.ds(mo(base, size), size)

    own_c = seg(c * q1, q1)
    oth_c = seg((1 - c) * q1, q1)
    keep1 = (seg(c * q1 + xc * q2, q2), seg(c * q1 + yc * q2, q2))
    send1 = (seg(c * q1 + (1 - xc) * q2, q2), seg(c * q1 + (1 - yc) * q2, q2))
    r_keep = (seg(yc * q3, q3), seg(xc * q3, q3))
    r_send = (seg((1 - yc) * q3, q3), seg((1 - xc) * q3, q3))
    colw = (slice(0, half), slice(half, FC))
    dev1, dev2 = (dev_x, dev_y), (dev_y, dev_x)
    g_c = (c * q1, (1 - c) * q1)
    g_keep1 = (c * q1 + xc * q2, c * q1 + yc * q2)
    g_send1 = (c * q1 + (1 - xc) * q2, c * q1 + (1 - yc) * q2)
    g_fin = (g_keep1[0] + yc * q3, g_keep1[1] + xc * q3)
    g_fin_n = (g_keep1[0] + (1 - yc) * q3, g_keep1[1] + (1 - xc) * q3)

    def gcols(j, r):
        return pl.ds(mo(f_of(j) * FC + r * half, half), half)

    def grows(j, off, size):
        return pl.ds(mo(base_of(j) + off, size), size)

    def ring(j):
        return lax.rem(j, RING)

    def d_copy(j):
        return remote(part.at[lax.rem(j, P_SLOTS), :, oth_c, :], dsum.at[lax.rem(j, D_SLOTS)],
                      ds.at[ring(j)], dr.at[ring(j)], dev_c)

    def p1_copy(j, r):
        return remote(part.at[lax.rem(j, P_SLOTS), :, send1[r], colw[r]], r1.at[j, r],
                      p1s.at[r, ring(j)], p1r.at[r, ring(j)], dev1[r])

    def p2_copy(j, r):
        return remote(r1.at[j, r, :, r_send[r], :], r2.at[j, r], p2s.at[r, ring(j)], p2r.at[r, ring(j)], dev2[r])

    def g1_copy(j, r, off):
        ref = gat.at[:, grows(j, off[r], q3), gcols(j, r)]
        return remote(ref, ref, g1s.at[r, ring(j)], g1r.at[r, ring(j)], dev2[r])

    def g2_copy(j, r, off):
        ref = gat.at[:, grows(j, off[r], q2), gcols(j, r)]
        return remote(ref, ref, g2s.at[r, ring(j)], g2r.at[r, ring(j)], dev1[r])

    def gd_copy(j, off):
        ref = gat.at[:, grows(j, off, q1), fcols(j)]
        return remote(ref, ref, gds.at[ring(j)], gdr.at[ring(j)], dev_c)

    def out_copy(j, k):
        dst = (a_hbm, du_hbm, dv_hbm)[k]
        return pltpu.make_async_copy(gat.at[k, trows(j), fcols(j)], dst.at[trows(j), fcols(j)], osem.at[k, ring(j)])

    z_sum = remote(acc.at[1], zin, zs.at[2], zr.at[2], dev_z)

    def step(i, carry):
        @pl.when(jnp.logical_and(i >= P_SLOTS, i < n_units + P_SLOTS))
        def _():
            j = i - P_SLOTS
            d_copy(j).wait_send()
            for r in range(2):
                p1_copy(j, r).wait_send()

        @pl.when(i < n_f)
        def _():
            for k in range(3):
                wcopy(k, i).wait()

        @pl.when(i == OWN_FIRST)
        def _():
            remote(dy_ref, dya_ref.at[oth, :], zs.at[0], zr.at[0], dev_z).wait_recv()
            h_copy(oth).wait_recv()

        @pl.when(i < n_units)
        def _():
            cs = fcols(i)
            slot = lax.rem(i, P_SLOTS)
            h = h_ref[trows(i), :]
            part[slot, 0] = jnp.dot(h, wg[:, cs], preferred_element_type=jnp.float32)
            part[slot, 1] = jnp.dot(h, wu[:, cs], preferred_element_type=jnp.float32)
            part[slot, 2] = contract_cols(dya_ref[trows(i), :], wd[cs, :])
            d_copy(i).start()

        @pl.when(jnp.logical_and(i >= 1, i < n_units + 1))
        def _():
            j = i - 1
            d_copy(j).wait_recv()
            slot = lax.rem(j, P_SLOTS)
            dslot = lax.rem(j, D_SLOTS)
            for k in range(3):
                part[slot, k, own_c, :] = part[slot, k, own_c, :] + dsum[dslot, k]
            for r in range(2):
                p1_copy(j, r).start()

        @pl.when(jnp.logical_and(i >= 2, i < n_units + 2))
        def _():
            j = i - 2
            slot = lax.rem(j, P_SLOTS)
            for r in range(2):
                p1_copy(j, r).wait_recv()
                for k in range(3):
                    r1[j, r, k] = r1[j, r, k] + part[slot, k, keep1[r], colw[r]]
                p2_copy(j, r).start()

        @pl.when(jnp.logical_and(i >= 3, i < n_units + 3))
        def _():
            j = i - 3
            for r in range(2):
                p2_copy(j, r).wait_recv()
                u = r1[j, r, 0, r_keep[r], :] + r2[j, r, 0]
                v = r1[j, r, 1, r_keep[r], :] + r2[j, r, 1]
                da = r1[j, r, 2, r_keep[r], :] + r2[j, r, 2]
                sig = jax.nn.sigmoid(u)
                swish = u * sig
                cs = gcols(j, r)
                rs = grows(j, g_fin[r], q3)
                gat[0, rs, cs] = (swish * v).astype(jnp.bfloat16)
                gat[1, rs, cs] = (da * v * sig * (1.0 + u * (1.0 - sig))).astype(jnp.bfloat16)
                gat[2, rs, cs] = (da * swish).astype(jnp.bfloat16)
                g1_copy(j, r, g_fin).start()

        @pl.when(jnp.logical_and(i >= 4, i < n_units + 4))
        def _():
            j = i - 4
            for r in range(2):
                g1_copy(j, r, g_fin_n).wait_recv()
                g2_copy(j, r, g_keep1).start()

        @pl.when(jnp.logical_and(i >= 5, i < n_units + 5))
        def _():
            j = i - 5
            for r in range(2):
                g2_copy(j, r, g_send1).wait_recv()
            gd_copy(j, g_c[0]).start()

        @pl.when(i >= 6)
        def _():
            j = i - 6
            gd_copy(j, g_c[1]).wait_recv()

            @pl.when(j >= RING)
            def _():
                for k in range(3):
                    out_copy(j - RING, k).wait()

            for k in range(3):
                out_copy(j, k).start()
            cs = fcols(j)
            rs = trows(j)
            side = oth_of(j)
            acc[side, 0] += jnp.dot(gat[0, rs, cs], wd[cs, :], preferred_element_type=jnp.float32)
            acc[side, 1] += contract_cols(gat[1, rs, cs], wg[:, cs]) + contract_cols(gat[2, rs, cs], wu[:, cs])
            for r in range(2):
                p2_copy(j, r).wait_send()
                g1_copy(j, r, g_fin).wait_send()
                g2_copy(j, r, g_keep1).wait_send()
            gd_copy(j, g_c[0]).wait_send()

            @pl.when(j == last_oth)
            def _():
                z_sum.start()
        return carry

    lax.fori_loop(0, n_units + 6, step, 0)

    z_sum.wait()
    d_hnorm = acc[0, 1] + zin[1]
    e = d_hnorm * gain
    rb[t] = pack_cols(jnp.sum(e, axis=1, keepdims=True), jnp.sum(e * xh[...], axis=1, keepdims=True))
    send_stats(rb, bs, br)
    dgs[...] = jnp.broadcast_to(jnp.sum(d_hnorm * xh[...], axis=0, keepdims=True), dgs.shape)
    z_dg = remote(dgs, dgr, zs.at[3], zr.at[3], dev_z)
    z_dg.start()
    zdy.wait_send()
    h_copy(own).wait_send()
    y_ref[...] = (x_ref[...].astype(jnp.float32) + (acc[0, 0] + zin[0])).astype(jnp.bfloat16)
    c0, c1 = total_stats(rb, bs, br)
    dx_ln = inv_std * (e - c0 / d_model - xh[...] * (c1 / d_model))
    dx_ref[...] = (dy_ref[...].astype(jnp.float32) + dx_ln).astype(jnp.bfloat16)
    z_dg.wait()
    dg_ref[...] = dgs[0:1, :] + dgr[0:1, :]

    def drain(j, carry):
        for k in range(3):
            out_copy(j, k).wait()
        return carry

    lax.fori_loop(n_units - RING, n_units, drain, 0)


def weight_grad_kernel(a_ref, du_ref, dv_ref, h_ref, dy_ref, y_in, dx_in, dg_in,
                       dwg_ref, dwu_ref, dwd_ref, y_ref, dx_ref, dg_ref, h_t):
    @pl.when(pl.program_id(0) == 0)
    def _():
        h_t[...] = h_ref[...].T
        y_ref[...] = y_in[...]
        dx_ref[...] = dx_in[...]
        dg_ref[...] = dg_in[...]

    dwg_ref[...] = jnp.dot(h_t[...], du_ref[...], preferred_element_type=jnp.float32)
    dwu_ref[...] = jnp.dot(h_t[...], dv_ref[...], preferred_element_type=jnp.float32)
    dwd_ref[...] = contract_rows(a_ref[...], dy_ref[...])


def solution(mesh):
    tx_size = mesh.shape["tx"]
    ty_size = mesh.shape["ty"]

    def local_step(x_blk, dy_blk, gain_blk, w_gate_blk, w_up_blk, w_down_blk):
        rows, dl = x_blk.shape
        fl = w_gate_blk.shape[1]
        tok = rows * ty_size
        d_model = dl * tx_size
        n = fl // FC
        half = FC // 2
        f32, bf16 = jnp.float32, jnp.bfloat16
        vm = pl.BlockSpec(memory_space=pltpu.VMEM)
        anyspec = pl.BlockSpec(memory_space=pl.ANY)
        sem = pltpu.SemaphoreType.DMA
        S = jax.ShapeDtypeStruct
        outs = pl.pallas_call(
            functools.partial(branch_kernel, d_model, n),
            out_shape=[S((tok, fl), bf16)] * 3 + [S((tok, dl), bf16)] * 2 + [S((rows, dl), bf16)] * 2 + [S((1, dl), f32)],
            in_specs=[vm] * 3 + [anyspec] * 3,
            out_specs=[anyspec] * 3 + [vm] * 5,
            scratch_shapes=[
                pltpu.VMEM((dl, fl), bf16), pltpu.VMEM((dl, fl), bf16), pltpu.VMEM((fl, dl), bf16),
                pltpu.VMEM((rows, dl), f32),
                pltpu.VMEM((P_SLOTS, 3, rows, FC), f32),
                pltpu.VMEM((D_SLOTS, 3, rows // 2, FC), f32),
                pltpu.VMEM((2 * n, 2, 3, rows // 4, half), f32),
                pltpu.VMEM((2 * n, 2, 3, rows // 8, half), f32),
                pltpu.VMEM((3, tok, fl), bf16),
                pltpu.VMEM((2, 2, rows, dl), f32), pltpu.VMEM((2, rows, dl), f32),
                pltpu.VMEM((8, 8, 128), f32), pltpu.VMEM((8, 8, 128), f32),
                pltpu.VMEM((8, dl), f32), pltpu.VMEM((8, dl), f32),
                sem((3, n)), sem((4,)), sem((4,)), sem((8,)), sem((8,)), sem((8,)), sem((8,)),
                sem((RING,)), sem((RING,)), sem((2, RING)), sem((2, RING)), sem((2, RING)), sem((2, RING)),
                sem((2, RING)), sem((2, RING)), sem((2, RING)), sem((2, RING)), sem((RING,)), sem((RING,)), sem((3, RING)),
            ],
            compiler_params=pltpu.CompilerParams(collective_id=0, has_side_effects=True, vmem_limit_bytes=62 * 1024 * 1024),
            cost_estimate=pl.CostEstimate(flops=12 * tok * dl * fl, bytes_accessed=6 * dl * fl + 6 * tok * fl, transcendentals=0),
        )(x_blk, dy_blk, gain_blk[None, :], w_gate_blk, w_up_blk, w_down_blk)

        kf = 512
        whole = lambda shape: pl.BlockSpec(shape, lambda i: (0, 0))
        cols = pl.BlockSpec((tok, kf), lambda i: (0, i))
        dwg, dwu, dwd, y_blk, dx_blk, dg = pl.pallas_call(
            weight_grad_kernel,
            grid=(fl // kf,),
            out_shape=[S((dl, fl), f32)] * 2 + [S((fl, dl), f32)] + [S((rows, dl), bf16)] * 2 + [S((1, dl), f32)],
            in_specs=[cols] * 3 + [whole((tok, dl))] * 2 + [whole((rows, dl))] * 2 + [whole((1, dl))],
            out_specs=[pl.BlockSpec((dl, kf), lambda i: (0, i))] * 2 + [pl.BlockSpec((kf, dl), lambda i: (i, 0))]
            + [whole((rows, dl))] * 2 + [whole((1, dl))],
            scratch_shapes=[pltpu.VMEM((dl, tok), bf16)],
            compiler_params=pltpu.CompilerParams(dimension_semantics=("arbitrary",), vmem_limit_bytes=48 * 1024 * 1024),
            cost_estimate=pl.CostEstimate(flops=6 * tok * dl * fl, bytes_accessed=12 * dl * fl + 6 * tok * fl, transcendentals=0),
        )(*outs)
        return (y_blk, dx_blk, dwg, dwu, dwd, dg[0])

    return jax.shard_map(
        local_step, mesh=mesh,
        in_specs=(P("ty", "tx"), P("ty", "tx"), P("tx"), P("tx", "ty"), P("tx", "ty"), P("ty", "tx")),
        out_specs=(P("ty", "tx"), P("ty", "tx"), P("tx", "ty"), P("tx", "ty"), P("ty", "tx"), P("tx")),
        check_vma=False)
```

time: 216 us -> 205 us (0.949)
  matrix products: 28 us -> 0 us
  Pallas kernels: 182 us -> 197 us
  local copies, waits for them, and re-layouts: 0.28 us -> 6.56 us
  starting transfers between devices: 2.83 us -> 0 us
    dot_general x3 -> x0, matrix products: 28 us -> none  [contract_rows(): lax.dot_general(left_op, right_op, (((0,), (0,)), ((), ())), preferred_el...]
    pallas_call x0 -> x1, Pallas kernels: none -> 20.7 us  [local_step(): pl.pallas_call(weight_grad_kernel, grid=(fl // kf,), out_shape=[S((dl, fl...]
    unnamed x22 -> x12, local copies, waits for them, and re-layouts: 0.05 us -> 6.56 us
    pallas_call x1, Pallas kernels: 182 us -> 176 us  [local_step(): pl.pallas_call(functools.partial(branch_kernel, d_model, n), out_shape=[S...]
    ppermute x3 -> x0, starting transfers between devices: 2.83 us -> none  [the longest x1 1.26 us: local_step(): m_in = lax.ppermute(m_oth, 'ty', swap)]
  transfers between devices with their start and end apart: 3 -> 0, of which waited for: 0 -> 0; matrix products, arithmetic and copies ran while one was open for 13% -> 0% of each run, Pallas kernels for 0% -> 0%
where the time goes in v2:
time: 205 us; the launch traced here: 204 us
  Pallas kernels  197 us (96%)
  local copies, waits for them, and re-layouts  6.56 us (3%)
    pallas_call x1, Pallas kernels, local_step(): pl.pallas_call(functools.partial(branch_kernel, d_model, n), out_shape=[S...  176 us
    pallas_call x1, Pallas kernels, local_step(): pl.pallas_call(weight_grad_kernel, grid=(fl // kf,), out_shape=[S((dl, fl...  20.7 us
    unnamed x12, local copies, waits for them, and re-layouts  6.56 us

profile of v2, /device:TPU:0, one launch (start us, length us, event | category | flops | bytes accessed | tf_op | source)
XLA Modules:
  0.0 204.1 jit_solution(14335574912449754878)
XLA Ops:
  0.6 176.2 %shard_map.109 = (bf16[256,8192]{1,0:T(8,128)(2,1)}, bf16[256,8192]{1,0:T(8,128)(2,1)}, bf16[256,8192]{1,0:T(8,128)(2,1)}, bf16[256,512]{1,0:T(8,128)(2,1)}, bf1...) custom-call(bf16[128,512]{1,0:T(8,128)(2,1)} %x_ref.1, ...), custom_call_target="tpu_custom_call" | custom-call | flops 12884901888 | bytes 37748736 | tf_op jit(solution)/shard_map/pallas_call | solution.py:361
  176.8 0.0 copy-start
  176.8 2.2 %copy-done = bf16[256,8192]{1,0:T(8,128)(2,1)S(1)} copy-done((bf16[256,8192]{1,0:T(8,128)(2,1)S(1)}, bf16[256,8192]{1,0:T(8,128)(2,1)}, u32[]{:S(2)}) %copy-start) | copy-done | bytes 4194328
  179.0 0.0 copy-start.1
  179.0 0.9 copy-done.1
  180.0 0.0 copy-start.2
  180.0 0.9 copy-done.2
  180.9 0.0 copy-start.3
  180.9 0.9 copy-done.3
  181.8 0.0 copy-start.4
  181.8 0.9 copy-done.4
  182.7 0.0 copy-start.5
  182.7 0.7 copy-done.5
  183.4 20.7 %shard_map.110 = (f32[512,8192]{1,0:T(8,128)}, f32[512,8192]{1,0:T(8,128)}, f32[8192,512]{1,0:T(8,128)}, bf16[128,512]{1,0:T(8,128)(2,1)}, bf16[128,512]{1,0:T(8,128)(2,1)}, /*index=5*/f32[1,512]{1,0:T(1,128)}) custom-call(bf16[256,8192]{1,0:T(8,128)(2,1)S(1)} %copy-done, bf16[256,8192]{1,0:T(8,128)(2,1)} %get-tuple-element.21.du_ref, ...), custom_call_target="tpu_custom_call" | custom-call | flops 6442450944 | bytes 62914560 | tf_op jit(solution)/shard_map/pallas_call | solution.py:388
Async XLA Ops:
  176.8 2.2 %copy-start = (bf16[256,8192]{1,0:T(8,128)(2,1)S(1)}, bf16[256,8192]{1,0:T(8,128)(2,1)}, u32[]{:S(2)}) copy-start(bf16[256,8192]{1,0:T(8,128)(2,1)} %get-tuple-element.20.a_ref) | copy-start | bytes 12582916
  179.0 0.9 copy-start.1
  180.0 0.9 copy-start.2
  180.9 0.9 copy-start.3
  181.8 0.9 copy-start.4
  182.7 0.7 copy-start.5

commit v3 on v2

v3 whole, which is shorter than its diff:
```python
import functools

import jax
import jax.numpy as jnp
from jax import lax
from jax.experimental import pallas as pl
from jax.experimental.pallas import tpu as pltpu
from jax.sharding import PartitionSpec as P

LN_EPS = 1e-6
MESH = pl.DeviceIdType.MESH
FC = 512
OWN_FIRST = 8
LEAD = 6
P_SLOTS = 4
L_SLOTS = LEAD + P_SLOTS
RING = 16
STAGES = (1, 3, 5, 7, 9, 10)
WB = 512
W_SLOTS = 3
VMEM_LIMIT = 62 * 1024 * 1024


def contract_rows(left_op, right_op):
    return lax.dot_general(left_op, right_op, (((0,), (0,)), ((), ())), preferred_element_type=jnp.float32)


def contract_cols(left_op, right_op):
    return lax.dot_general(left_op, right_op, (((1,), (1,)), ((), ())), preferred_element_type=jnp.float32)


def mo(value, multiple):
    return pl.multiple_of(value, multiple)


def branch_kernel(d_model, n_f,
                  x_hbm, dy_hbm, gain_hbm, wg_hbm, wu_hbm, wd_hbm,
                  a_hbm, du_hbm, dv_hbm, h_hbm, dya_hbm, y_hbm, dx_hbm, dg_hbm,
                  x_ref, gain_ref, h_ref, dya_ref, y_ref, dx_ref, dg_ref,
                  wg, wu, wd, xh, part, part_d, dsum, dsum_d, r1, r2, gat, acc, zin, st, rb, dgs, dgr,
                  wsem, isem, zs, zr, ss, sr, bs, br, ds, dr, dds, ddr, p1s, p1r, pds, pdr, p2s, p2r,
                  g1s, g1r, g2s, g2r, gds, gdr, osem, fsem):
    half = FC // 2
    rows = x_ref.shape[0]
    q1, q2, q3 = rows // 2, rows // 4, rows // 8
    n_units = 2 * n_f
    last_oth = OWN_FIRST + n_f - 1

    ty = lax.axis_index("ty")
    t = lax.axis_index("tx")
    c = lax.rem(t, 2)
    xc = lax.rem(lax.div(t, 2), 2)
    yc = lax.div(t, 4)
    dev_c = (ty, t + 1 - 2 * c)
    dev_x = (ty, t + 2 - 4 * xc)
    dev_y = (ty, t + 4 - 8 * yc)
    dev_z = (1 - ty, t)
    own = pl.ds(mo(ty * rows, rows), rows)
    oth = pl.ds(mo((1 - ty) * rows, rows), rows)

    def remote(src, dst, ssem, rsem, dev):
        return pltpu.make_async_remote_copy(src_ref=src, dst_ref=dst, send_sem=ssem, recv_sem=rsem,
                                            device_id=dev, device_id_type=MESH)

    def f_of(j):
        return lax.rem(j + (n_f - OWN_FIRST), n_f)

    def oth_of(j):
        return lax.rem(lax.div(j + (n_f - OWN_FIRST), n_f), 2)

    def base_of(j):
        k = oth_of(j)
        return (ty + k - 2 * ty * k) * rows

    def fcols(j):
        return pl.ds(mo(f_of(j) * FC, FC), FC)

    def trows(j):
        return pl.ds(mo(base_of(j), rows), rows)

    def wcopy(k, i):
        cs = fcols(i)
        if k == 0:
            return pltpu.make_async_copy(wg_hbm.at[:, cs], wg.at[:, cs], wsem.at[0, i])
        if k == 1:
            return pltpu.make_async_copy(wu_hbm.at[:, cs], wu.at[:, cs], wsem.at[1, i])
        return pltpu.make_async_copy(wd_hbm.at[cs, :], wd.at[cs, :], wsem.at[2, i])

    in_dy = pltpu.make_async_copy(dy_hbm, dya_ref.at[own, :], isem.at[0])
    in_x = pltpu.make_async_copy(x_hbm, x_ref, isem.at[1])
    in_gain = pltpu.make_async_copy(gain_hbm, gain_ref, isem.at[2])
    in_x.start()
    in_dy.start()
    in_gain.start()
    for i in range(LEAD):
        wcopy(2, i).start()

    barrier = pltpu.get_barrier_semaphore()
    for o in range(1, 8):
        pl.semaphore_signal(barrier, inc=1, device_id=(ty, lax.rem(t + o, 8)), device_id_type=MESH)
    pl.semaphore_signal(barrier, inc=1, device_id=dev_z, device_id_type=MESH)

    def start_w(i, carry):
        wcopy(0, i).start()
        wcopy(1, i).start()

        @pl.when(i + LEAD < n_f)
        def _():
            wcopy(2, i + LEAD).start()
        return carry

    lax.fori_loop(0, n_f, start_w, 0)

    lane = lax.broadcasted_iota(jnp.int32, (rows, 128), 1)

    def pack_cols(c0, c1):
        both = jnp.where(lane == 0, c0, jnp.where(lane == 1, c1, 0.0))
        return both.T[0:8, :]

    def unpack_cols(packed):
        full = jnp.concatenate([packed, jnp.zeros((rows - 8, 128), jnp.float32)], axis=0).T
        return full[:, 0:1], full[:, 1:2]

    def send_stats(buf, ssem, rsem):
        for o in range(1, 8):
            remote(buf.at[t], buf.at[t], ssem.at[o], rsem.at[o], (ty, lax.rem(t + o, 8))).start()

    def total_stats(buf, ssem, rsem):
        for o in range(1, 8):
            q = lax.rem(t + 8 - o, 8)
            d = remote(buf.at[t], buf.at[q], ssem.at[o], rsem.at[o], (ty, q))
            d.wait_send()
            d.wait_recv()
        s = buf[0]
        for j in range(1, 8):
            s = s + buf[j]
        return unpack_cols(s)

    def seg(base, size):
        return pl.ds(mo(base, size), size)

    own_c = seg(c * q1, q1)
    oth_c = seg((1 - c) * q1, q1)
    keep1 = (seg(c * q1 + xc * q2, q2), seg(c * q1 + yc * q2, q2))
    send1 = (seg(c * q1 + (1 - xc) * q2, q2), seg(c * q1 + (1 - yc) * q2, q2))
    r_keep = (seg(yc * q3, q3), seg(xc * q3, q3))
    r_send = (seg((1 - yc) * q3, q3), seg((1 - xc) * q3, q3))
    colw = (slice(0, half), slice(half, FC))
    dev1, dev2 = (dev_x, dev_y), (dev_y, dev_x)
    g_c = (c * q1, (1 - c) * q1)
    g_keep1 = (c * q1 + xc * q2, c * q1 + yc * q2)
    g_send1 = (c * q1 + (1 - xc) * q2, c * q1 + (1 - yc) * q2)
    g_fin = (g_keep1[0] + yc * q3, g_keep1[1] + xc * q3)
    g_fin_n = (g_keep1[0] + (1 - yc) * q3, g_keep1[1] + (1 - xc) * q3)

    def gcols(j, r):
        return pl.ds(mo(f_of(j) * FC + r * half, half), half)

    def grows(j, off, size):
        return pl.ds(mo(base_of(j) + off, size), size)

    def ring(j):
        return lax.rem(j, RING)

    def d_copy(j):
        slot = lax.rem(j, P_SLOTS)
        return remote(part.at[slot, :, oth_c, :], dsum.at[slot], ds.at[ring(j)], dr.at[ring(j)], dev_c)

    def dd_copy(j):
        slot = lax.rem(j, L_SLOTS)
        return remote(part_d.at[slot, oth_c, :], dsum_d.at[slot], dds.at[ring(j)], ddr.at[ring(j)], dev_c)

    def p1_copy(j, r):
        return remote(part.at[lax.rem(j, P_SLOTS), :, send1[r], colw[r]], r1.at[j, r, 0:2],
                      p1s.at[r, ring(j)], p1r.at[r, ring(j)], dev1[r])

    def pd_copy(j, r):
        return remote(part_d.at[lax.rem(j, L_SLOTS), send1[r], colw[r]], r1.at[j, r, 2],
                      pds.at[r, ring(j)], pdr.at[r, ring(j)], dev1[r])

    def p2_copy(j, r):
        return remote(r1.at[j, r, :, r_send[r], :], r2.at[j, r], p2s.at[r, ring(j)], p2r.at[r, ring(j)], dev2[r])

    def g1_copy(j, r, off):
        ref = gat.at[:, grows(j, off[r], q3), gcols(j, r)]
        return remote(ref, ref, g1s.at[r, ring(j)], g1r.at[r, ring(j)], dev2[r])

    def g2_copy(j, r, off):
        ref = gat.at[:, grows(j, off[r], q2), gcols(j, r)]
        return remote(ref, ref, g2s.at[r, ring(j)], g2r.at[r, ring(j)], dev1[r])

    def gd_copy(j, off):
        ref = gat.at[:, grows(j, off, q1), fcols(j)]
        return remote(ref, ref, gds.at[ring(j)], gdr.at[ring(j)], dev_c)

    def out_copy(j, k):
        dst = (a_hbm, du_hbm, dv_hbm)[k]
        return pltpu.make_async_copy(gat.at[k, trows(j), fcols(j)], dst.at[trows(j), fcols(j)], osem.at[k, ring(j)])

    def da_product(j):
        part_d[lax.rem(j, L_SLOTS)] = contract_cols(dya_ref[trows(j), :], wd[fcols(j), :])
        dd_copy(j).start()

    def da_pair_sum(j):
        dd_copy(j).wait_recv()
        slot = lax.rem(j, L_SLOTS)
        part_d[slot, own_c, :] = part_d[slot, own_c, :] + dsum_d[slot]
        for r in range(2):
            pd_copy(j, r).start()

    in_x.wait()
    x_own = x_ref[...].astype(jnp.float32)
    st[t] = pack_cols(jnp.sum(x_own, axis=1, keepdims=True), jnp.sum(x_own * x_own, axis=1, keepdims=True))
    in_dy.wait()
    in_gain.wait()
    pl.semaphore_wait(barrier, 8)
    send_stats(st, ss, sr)
    zdy = remote(dya_ref.at[own, :], dya_ref.at[own, :], zs.at[0], zr.at[0], dev_z)
    zdy.start()
    for i in range(LEAD):
        wcopy(2, i).wait()
        da_product(i)
    for i in range(LEAD):
        da_pair_sum(i)
    acc[...] = jnp.zeros_like(acc)

    gain = gain_ref[...]
    c0, c1 = total_stats(st, ss, sr)
    mean_x = c0 / d_model
    inv_std = lax.rsqrt(c1 / d_model - mean_x * mean_x + LN_EPS)
    xhat = (x_ref[...].astype(jnp.float32) - mean_x) * inv_std
    xh[...] = xhat
    h_ref[own, :] = (gain * xhat).astype(jnp.bfloat16)

    def h_copy(block):
        return remote(h_ref.at[own, :], h_ref.at[block, :], zs.at[1], zr.at[1], dev_z)

    h_copy(own).start()

    z_sum = remote(acc.at[1], zin, zs.at[2], zr.at[2], dev_z)
    h_out = pltpu.make_async_copy(h_ref, h_hbm, fsem.at[0])
    dya_out = pltpu.make_async_copy(dya_ref, dya_hbm, fsem.at[1])

    def step(i, carry):
        @pl.when(jnp.logical_and(i >= P_SLOTS, i < n_units + P_SLOTS))
        def _():
            j = i - P_SLOTS
            d_copy(j).wait_send()
            dd_copy(j).wait_send()
            for r in range(2):
                p1_copy(j, r).wait_send()
                pd_copy(j, r).wait_send()

        @pl.when(i < n_f)
        def _():
            wcopy(0, i).wait()
            wcopy(1, i).wait()

        @pl.when(i + LEAD < n_f)
        def _():
            wcopy(2, i + LEAD).wait()

        @pl.when(i == OWN_FIRST - LEAD)
        def _():
            remote(dya_ref.at[own, :], dya_ref.at[oth, :], zs.at[0], zr.at[0], dev_z).wait_recv()
            dya_out.start()

        @pl.when(i == OWN_FIRST)
        def _():
            h_copy(oth).wait_recv()
            h_out.start()

        @pl.when(i < n_units)
        def _():
            cs = fcols(i)
            slot = lax.rem(i, P_SLOTS)
            h = h_ref[trows(i), :]
            part[slot, 0] = jnp.dot(h, wg[:, cs], preferred_element_type=jnp.float32)
            part[slot, 1] = jnp.dot(h, wu[:, cs], preferred_element_type=jnp.float32)
            d_copy(i).start()

        @pl.when(i + LEAD < n_units)
        def _():
            da_product(i + LEAD)

        @pl.when(jnp.logical_and(i >= STAGES[0], i < n_units + STAGES[0]))
        def _():
            j = i - STAGES[0]
            d_copy(j).wait_recv()
            slot = lax.rem(j, P_SLOTS)
            for k in range(2):
                part[slot, k, own_c, :] = part[slot, k, own_c, :] + dsum[slot, k]
            for r in range(2):
                p1_copy(j, r).start()

            @pl.when(j + LEAD < n_units)
            def _():
                da_pair_sum(j + LEAD)

        @pl.when(jnp.logical_and(i >= STAGES[1], i < n_units + STAGES[1]))
        def _():
            j = i - STAGES[1]
            slot = lax.rem(j, P_SLOTS)
            for r in range(2):
                pd_copy(j, r).wait_recv()
                p1_copy(j, r).wait_recv()
                for k in range(2):
                    r1[j, r, k] = r1[j, r, k] + part[slot, k, keep1[r], colw[r]]
                r1[j, r, 2] = r1[j, r, 2] + part_d[lax.rem(j, L_SLOTS), keep1[r], colw[r]]
                p2_copy(j, r).start()

        @pl.when(jnp.logical_and(i >= STAGES[2], i < n_units + STAGES[2]))
        def _():
            j = i - STAGES[2]
            for r in range(2):
                p2_copy(j, r).wait_recv()
                u = r1[j, r, 0, r_keep[r], :] + r2[j, r, 0]
                v = r1[j, r, 1, r_keep[r], :] + r2[j, r, 1]
                da = r1[j, r, 2, r_keep[r], :] + r2[j, r, 2]
                sig = jax.nn.sigmoid(u)
                swish = u * sig
                cs = gcols(j, r)
                rs = grows(j, g_fin[r], q3)
                gat[0, rs, cs] = (swish * v).astype(jnp.bfloat16)
                gat[1, rs, cs] = (da * v * sig * (1.0 + u * (1.0 - sig))).astype(jnp.bfloat16)
                gat[2, rs, cs] = (da * swish).astype(jnp.bfloat16)
                g1_copy(j, r, g_fin).start()

        @pl.when(jnp.logical_and(i >= STAGES[3], i < n_units + STAGES[3]))
        def _():
            j = i - STAGES[3]
            for r in range(2):
                g1_copy(j, r, g_fin_n).wait_recv()
                g2_copy(j, r, g_keep1).start()

        @pl.when(jnp.logical_and(i >= STAGES[4], i < n_units + STAGES[4]))
        def _():
            j = i - STAGES[4]
            for r in range(2):
                g2_copy(j, r, g_send1).wait_recv()
            gd_copy(j, g_c[0]).start()

        @pl.when(i >= STAGES[5])
        def _():
            j = i - STAGES[5]
            gd_copy(j, g_c[1]).wait_recv()

            @pl.when(j >= RING)
            def _():
                for k in range(3):
                    out_copy(j - RING, k).wait()

            for k in range(3):
                out_copy(j, k).start()
            cs = fcols(j)
            rs = trows(j)
            side = oth_of(j)
            acc[side, 0] += jnp.dot(gat[0, rs, cs], wd[cs, :], preferred_element_type=jnp.float32)
            acc[side, 1] += contract_cols(gat[1, rs, cs], wg[:, cs]) + contract_cols(gat[2, rs, cs], wu[:, cs])
            for r in range(2):
                p2_copy(j, r).wait_send()
                g1_copy(j, r, g_fin).wait_send()
                g2_copy(j, r, g_keep1).wait_send()
            gd_copy(j, g_c[0]).wait_send()

            @pl.when(j == last_oth)
            def _():
                z_sum.start()
        return carry

    lax.fori_loop(0, n_units + STAGES[5], step, 0)

    z_sum.wait()
    d_hnorm = acc[0, 1] + zin[1]
    e = d_hnorm * gain
    rb[t] = pack_cols(jnp.sum(e, axis=1, keepdims=True), jnp.sum(e * xh[...], axis=1, keepdims=True))
    send_stats(rb, bs, br)
    dgs[...] = jnp.broadcast_to(jnp.sum(d_hnorm * xh[...], axis=0, keepdims=True), dgs.shape)
    z_dg = remote(dgs, dgr, zs.at[3], zr.at[3], dev_z)
    z_dg.start()
    y_ref[...] = (x_ref[...].astype(jnp.float32) + (acc[0, 0] + zin[0])).astype(jnp.bfloat16)
    y_out = pltpu.make_async_copy(y_ref, y_hbm, fsem.at[2])
    y_out.start()
    zdy.wait_send()
    h_copy(own).wait_send()
    h_out.wait()
    dya_out.wait()

    def drain(j, carry):
        for k in range(3):
            out_copy(j, k).wait()
        return carry

    lax.fori_loop(n_units - RING, n_units, drain, 0)
    c0, c1 = total_stats(rb, bs, br)
    dx_ln = inv_std * (e - c0 / d_model - xh[...] * (c1 / d_model))
    dx_ref[...] = (dya_ref[own, :].astype(jnp.float32) + dx_ln).astype(jnp.bfloat16)
    dx_out = pltpu.make_async_copy(dx_ref, dx_hbm, fsem.at[3])
    dx_out.start()
    z_dg.wait()
    dg_ref[...] = dgs[0:1, :] + dgr[0:1, :]
    dg_out = pltpu.make_async_copy(dg_ref, dg_hbm, fsem.at[4])
    dg_out.start()
    y_out.wait()
    dx_out.wait()
    dg_out.wait()


def weight_grad_kernel(a_hbm, du_hbm, dv_hbm, h_hbm, dy_hbm, y_in, dx_in, dg_in,
                       dwg_hbm, dwu_hbm, dwd_hbm, y_hbm, dx_hbm, dg_hbm,
                       h_ref, dy_ref, h_t, y_ref, dx_ref, dg_ref, ins, buf, isem, bsem, ssem):
    n_blocks = a_hbm.shape[1] // WB

    def in_copy(b, k):
        slot = lax.rem(b, W_SLOTS)
        src = (a_hbm, du_hbm, dv_hbm)[k].at[:, pl.ds(mo(b * WB, WB), WB)]
        return pltpu.make_async_copy(src, ins.at[slot, k], isem.at[slot, k])

    def out_copy(b, k):
        cs = pl.ds(mo(b * WB, WB), WB)
        dst = (dwg_hbm.at[:, cs], dwu_hbm.at[:, cs], dwd_hbm.at[cs, :])[k]
        slot = lax.rem(b, W_SLOTS)
        return pltpu.make_async_copy(buf.at[slot, k], dst, bsem.at[slot, k])

    h_in = pltpu.make_async_copy(h_hbm, h_ref, ssem.at[0])
    dy_in = pltpu.make_async_copy(dy_hbm, dy_ref, ssem.at[1])
    small_in = [pltpu.make_async_copy(src, dst, ssem.at[2 + k])
                for k, (src, dst) in enumerate(((y_in, y_ref), (dx_in, dx_ref), (dg_in, dg_ref)))]
    small_out = [pltpu.make_async_copy(src, dst, ssem.at[5 + k])
                 for k, (src, dst) in enumerate(((y_ref, y_hbm), (dx_ref, dx_hbm), (dg_ref, dg_hbm)))]
    h_in.start()
    for k in (1, 2, 0):
        in_copy(0, k).start()
    dy_in.start()
    for b in range(1, W_SLOTS):
        for k in range(3):
            in_copy(b, k).start()
    for d in small_in:
        d.start()
    h_in.wait()
    h_t[...] = h_ref[...].T
    dy_in.wait()

    def block(b, carry):
        slot = lax.rem(b, W_SLOTS)
        for k in range(3):
            src = (1, 2, 0)[k]

            @pl.when(b >= W_SLOTS)
            def _():
                out_copy(b - W_SLOTS, k).wait()

            in_copy(b, src).wait()
            if k < 2:
                buf[slot, k] = jnp.dot(h_t[...], ins[slot, src], preferred_element_type=jnp.float32)
            else:
                buf[slot, k] = contract_rows(ins[slot, src], dy_ref[...])
            out_copy(b, k).start()

            @pl.when(b + W_SLOTS < n_blocks)
            def _():
                in_copy(b + W_SLOTS, src).start()
        return carry

    lax.fori_loop(0, n_blocks, block, 0)
    for d in small_in:
        d.wait()
    for d in small_out:
        d.start()

    def drain(b, carry):
        for k in range(3):
            out_copy(b, k).wait()
        return carry

    lax.fori_loop(n_blocks - W_SLOTS, n_blocks, drain, 0)
    for d in small_out:
        d.wait()


def solution(mesh):
    tx_size = mesh.shape["tx"]
    ty_size = mesh.shape["ty"]

    def local_step(x_blk, dy_blk, gain_blk, w_gate_blk, w_up_blk, w_down_blk):
        rows, dl = x_blk.shape
        fl = w_gate_blk.shape[1]
        tok = rows * ty_size
        d_model = dl * tx_size
        n = fl // FC
        half = FC // 2
        f32, bf16 = jnp.float32, jnp.bfloat16
        anyspec = pl.BlockSpec(memory_space=pl.ANY)
        sem = pltpu.SemaphoreType.DMA
        S = jax.ShapeDtypeStruct
        V = pltpu.VMEM
        small = [((rows, dl), bf16), ((rows, dl), bf16), ((1, dl), f32)]
        outs = pl.pallas_call(
            functools.partial(branch_kernel, d_model, n),
            out_shape=[S((tok, fl), bf16)] * 3 + [S((tok, dl), bf16)] * 2 + [S(*s) for s in small],
            in_specs=[anyspec] * 6,
            out_specs=[anyspec] * 8,
            scratch_shapes=[
                V((rows, dl), bf16), V((1, dl), f32), V((tok, dl), bf16), V((tok, dl), bf16), *[V(*s) for s in small],
                V((dl, fl), bf16), V((dl, fl), bf16), V((fl, dl), bf16),
                V((rows, dl), f32),
                V((P_SLOTS, 2, rows, FC), f32), V((L_SLOTS, rows, FC), f32),
                V((P_SLOTS, 2, rows // 2, FC), f32), V((L_SLOTS, rows // 2, FC), f32),
                V((2 * n, 2, 3, rows // 4, half), f32), V((2 * n, 2, 3, rows // 8, half), f32),
                V((3, tok, fl), bf16),
                V((2, 2, rows, dl), f32), V((2, rows, dl), f32),
                V((8, 8, 128), f32), V((8, 8, 128), f32), V((8, dl), f32), V((8, dl), f32),
                sem((3, n)), sem((3,)), sem((4,)), sem((4,)), sem((8,)), sem((8,)), sem((8,)), sem((8,)),
                sem((RING,)), sem((RING,)), sem((RING,)), sem((RING,)),
                *[sem((2, RING)) for _ in range(10)],
                sem((RING,)), sem((RING,)), sem((3, RING)), sem((5,)),
            ],
            compiler_params=pltpu.CompilerParams(collective_id=0, has_side_effects=True, vmem_limit_bytes=VMEM_LIMIT),
            cost_estimate=pl.CostEstimate(flops=12 * tok * dl * fl, bytes_accessed=6 * dl * fl + 6 * tok * fl, transcendentals=0),
        )(x_blk, dy_blk, gain_blk[None, :], w_gate_blk, w_up_blk, w_down_blk)

        dwg, dwu, dwd, y_blk, dx_blk, dg = pl.pallas_call(
            weight_grad_kernel,
            out_shape=[S((dl, fl), f32)] * 2 + [S((fl, dl), f32)] + [S(*s) for s in small],
            in_specs=[anyspec] * 8,
            out_specs=[anyspec] * 6,
            scratch_shapes=[
                V((tok, dl), bf16), V((tok, dl), bf16), V((dl, tok), bf16), *[V(*s) for s in small],
                V((W_SLOTS, 3, tok, WB), bf16), V((W_SLOTS, 3, dl, WB), f32),
                sem((W_SLOTS, 3)), sem((W_SLOTS, 3)), sem((8,)),
            ],
            compiler_params=pltpu.CompilerParams(vmem_limit_bytes=VMEM_LIMIT),
            cost_estimate=pl.CostEstimate(flops=6 * tok * dl * fl, bytes_accessed=12 * dl * fl + 6 * tok * fl, transcendentals=0),
        )(*outs)
        return (y_blk, dx_blk, dwg, dwu, dwd, dg[0])

    return jax.shard_map(
        local_step, mesh=mesh,
        in_specs=(P("ty", "tx"), P("ty", "tx"), P("tx"), P("tx", "ty"), P("tx", "ty"), P("ty", "tx")),
        out_specs=(P("ty", "tx"), P("ty", "tx"), P("tx", "ty"), P("tx", "ty"), P("ty", "tx"), P("tx")),
        check_vma=False)
```

time: 205 us -> 193 us (0.941)
  local copies, waits for them, and re-layouts: 6.56 us -> 0 us
  Pallas kernels: 197 us -> 192 us
    unnamed x12 -> x0, local copies, waits for them, and re-layouts: 6.56 us -> none
    pallas_call x1, Pallas kernels: 176 us -> 171 us  [local_step(): pl.pallas_call(functools.partial(branch_kernel, d_model, n), out_shape=[S...]
where the time goes in v3:
time: 193 us
  Pallas kernels  192 us (99%)
    pallas_call x1, Pallas kernels, local_step(): pl.pallas_call(functools.partial(branch_kernel, d_model, n), out_shape=[S...  171 us
    pallas_call x1, Pallas kernels, local_step(): pl.pallas_call(weight_grad_kernel, out_shape=[S((dl, fl), f32)] * 2 + [S(...  21.1 us

profile of v3, /device:TPU:0, one launch (start us, length us, event | category | flops | bytes accessed | tf_op | source)
XLA Modules:
  0.0 192.6 jit_solution(16821921796749246362)
XLA Ops:
  0.6 170.9 %shard_map.109 = (bf16[256,8192]{1,0:T(8,128)(2,1)}, bf16[256,8192]{1,0:T(8,128)(2,1)}, bf16[256,8192]{1,0:T(8,128)(2,1)}, bf16[256,512]{1,0:T(8,128)(2,1)}, bf1...) custom-call(bf16[128,512]{1,0:T(8,128)(2,1)} %x_hbm.1, ...), custom_call_target="tpu_custom_call" | custom-call | flops 12884901888 | bytes 37748736 | tf_op jit(solution)/shard_map/pallas_call | solution.py:498
  171.5 21.1 %shard_map.110 = (f32[512,8192]{1,0:T(8,128)}, f32[512,8192]{1,0:T(8,128)}, f32[8192,512]{1,0:T(8,128)}, bf16[128,512]{1,0:T(8,128)(2,1)}, bf16[128,512]{1,0:T(8,128)(2,1)}, /*index=5*/f32[1,512]{1,0:T(1,128)}) custom-call(bf16[256,8192]{1,0:T(8,128)(2,1)} %get-tuple-element.20.a_hbm, bf16[256,8192]{1,0:T(8,128)(2,1)} %get-tuple-element.21.du_hbm, ...), custom_call_target="tpu_custom_call" | custom-call | flops 6442450944 | bytes 62914560 | tf_op jit(solution)/shard_map/pallas_call | solution.py:522

commit v4 on v3

--- a/solution.py
+++ b/solution.py
@@ -18,7 +18,7 @@
 STAGES = (1, 3, 5, 7, 9, 10)
 WB = 512
 W_SLOTS = 3
-VMEM_LIMIT = 62 * 1024 * 1024
+VMEM_LIMIT = 44 * 1024 * 1024
 
 
 def contract_rows(left_op, right_op):
@@ -35,11 +35,11 @@
 
 def branch_kernel(d_model, n_f,
                   x_hbm, dy_hbm, gain_hbm, wg_hbm, wu_hbm, wd_hbm,
-                  a_hbm, du_hbm, dv_hbm, h_hbm, dya_hbm, y_hbm, dx_hbm, dg_hbm,
-                  x_ref, gain_ref, h_ref, dya_ref, y_ref, dx_ref, dg_ref,
-                  wg, wu, wd, xh, part, part_d, dsum, dsum_d, r1, r2, gat, acc, zin, st, rb, dgs, dgr,
+                  gat, h_t, dya_ref, y_ref, dx_ref, dg_ref,
+                  x_ref, gain_ref, h_ref,
+                  wg, wu, wd, xh, part, part_d, dsum, dsum_d, r1, r2, acc, zin, st, rb, dgs, dgr,
                   wsem, isem, zs, zr, ss, sr, bs, br, ds, dr, dds, ddr, p1s, p1r, pds, pdr, p2s, p2r,
-                  g1s, g1r, g2s, g2r, gds, gdr, osem, fsem):
+                  g1s, g1r, g2s, g2r, gds, gdr):
     half = FC // 2
     rows = x_ref.shape[0]
     q1, q2, q3 = rows // 2, rows // 4, rows // 8
@@ -192,10 +192,6 @@
     def gd_copy(j, off):
         ref = gat.at[:, grows(j, off, q1), fcols(j)]
         return remote(ref, ref, gds.at[ring(j)], gdr.at[ring(j)], dev_c)
-
-    def out_copy(j, k):
-        dst = (a_hbm, du_hbm, dv_hbm)[k]
-        return pltpu.make_async_copy(gat.at[k, trows(j), fcols(j)], dst.at[trows(j), fcols(j)], osem.at[k, ring(j)])
 
     def da_product(j):
         part_d[lax.rem(j, L_SLOTS)] = contract_cols(dya_ref[trows(j), :], wd[fcols(j), :])
@@ -238,8 +234,6 @@
     h_copy(own).start()
 
     z_sum = remote(acc.at[1], zin, zs.at[2], zr.at[2], dev_z)
-    h_out = pltpu.make_async_copy(h_ref, h_hbm, fsem.at[0])
-    dya_out = pltpu.make_async_copy(dya_ref, dya_hbm, fsem.at[1])
 
     def step(i, carry):
         @pl.when(jnp.logical_and(i >= P_SLOTS, i < n_units + P_SLOTS))
@@ -263,12 +257,11 @@
         @pl.when(i == OWN_FIRST - LEAD)
         def _():
             remote(dya_ref.at[own, :], dya_ref.at[oth, :], zs.at[0], zr.at[0], dev_z).wait_recv()
-            dya_out.start()
 
         @pl.when(i == OWN_FIRST)
         def _():
             h_copy(oth).wait_recv()
-            h_out.start()
+            h_t[...] = h_ref[...].T
 
         @pl.when(i < n_units)
         def _():
@@ -345,13 +338,6 @@
             j = i - STAGES[5]
             gd_copy(j, g_c[1]).wait_recv()
 
-            @pl.when(j >= RING)
-            def _():
-                for k in range(3):
-                    out_copy(j - RING, k).wait()
-
-            for k in range(3):
-                out_copy(j, k).start()
             cs = fcols(j)
             rs = trows(j)
             side = oth_of(j)
@@ -379,42 +365,18 @@
     z_dg = remote(dgs, dgr, zs.at[3], zr.at[3], dev_z)
     z_dg.start()
     y_ref[...] = (x_ref[...].astype(jnp.float32) + (acc[0, 0] + zin[0])).astype(jnp.bfloat16)
-    y_out = pltpu.make_async_copy(y_ref, y_hbm, fsem.at[2])
-    y_out.start()
     zdy.wait_send()
     h_copy(own).wait_send()
-    h_out.wait()
-    dya_out.wait()
-
-    def drain(j, carry):
-        for k in range(3):
-            out_copy(j, k).wait()
-        return carry
-
-    lax.fori_loop(n_units - RING, n_units, drain, 0)
     c0, c1 = total_stats(rb, bs, br)
     dx_ln = inv_std * (e - c0 / d_model - xh[...] * (c1 / d_model))
     dx_ref[...] = (dya_ref[own, :].astype(jnp.float32) + dx_ln).astype(jnp.bfloat16)
-    dx_out = pltpu.make_async_copy(dx_ref, dx_hbm, fsem.at[3])
-    dx_out.start()
     z_dg.wait()
     dg_ref[...] = dgs[0:1, :] + dgr[0:1, :]
-    dg_out = pltpu.make_async_copy(dg_ref, dg_hbm, fsem.at[4])
-    dg_out.start()
-    y_out.wait()
-    dx_out.wait()
-    dg_out.wait()
-
-
-def weight_grad_kernel(a_hbm, du_hbm, dv_hbm, h_hbm, dy_hbm, y_in, dx_in, dg_in,
-                       dwg_hbm, dwu_hbm, dwd_hbm, y_hbm, dx_hbm, dg_hbm,
-                       h_ref, dy_ref, h_t, y_ref, dx_ref, dg_ref, ins, buf, isem, bsem, ssem):
-    n_blocks = a_hbm.shape[1] // WB
-
-    def in_copy(b, k):
-        slot = lax.rem(b, W_SLOTS)
-        src = (a_hbm, du_hbm, dv_hbm)[k].at[:, pl.ds(mo(b * WB, WB), WB)]
-        return pltpu.make_async_copy(src, ins.at[slot, k], isem.at[slot, k])
+
+
+def weight_grad_kernel(gat, h_t, dy_ref, y_in, dx_in, dg_in,
+                       dwg_hbm, dwu_hbm, dwd_hbm, y_hbm, dx_hbm, dg_hbm, buf, bsem, ssem):
+    n_blocks = gat.shape[2] // WB
 
     def out_copy(b, k):
         cs = pl.ds(mo(b * WB, WB), WB)
@@ -422,50 +384,25 @@
         slot = lax.rem(b, W_SLOTS)
         return pltpu.make_async_copy(buf.at[slot, k], dst, bsem.at[slot, k])
 
-    h_in = pltpu.make_async_copy(h_hbm, h_ref, ssem.at[0])
-    dy_in = pltpu.make_async_copy(dy_hbm, dy_ref, ssem.at[1])
-    small_in = [pltpu.make_async_copy(src, dst, ssem.at[2 + k])
-                for k, (src, dst) in enumerate(((y_in, y_ref), (dx_in, dx_ref), (dg_in, dg_ref)))]
-    small_out = [pltpu.make_async_copy(src, dst, ssem.at[5 + k])
-                 for k, (src, dst) in enumerate(((y_ref, y_hbm), (dx_ref, dx_hbm), (dg_ref, dg_hbm)))]
-    h_in.start()
-    for k in (1, 2, 0):
-        in_copy(0, k).start()
-    dy_in.start()
-    for b in range(1, W_SLOTS):
-        for k in range(3):
-            in_copy(b, k).start()
-    for d in small_in:
-        d.start()
-    h_in.wait()
-    h_t[...] = h_ref[...].T
-    dy_in.wait()
-
     def block(b, carry):
+        cs = pl.ds(mo(b * WB, WB), WB)
         slot = lax.rem(b, W_SLOTS)
         for k in range(3):
-            src = (1, 2, 0)[k]
-
             @pl.when(b >= W_SLOTS)
             def _():
                 out_copy(b - W_SLOTS, k).wait()
 
-            in_copy(b, src).wait()
             if k < 2:
-                buf[slot, k] = jnp.dot(h_t[...], ins[slot, src], preferred_element_type=jnp.float32)
+                buf[slot, k] = jnp.dot(h_t[...], gat[k + 1, :, cs], preferred_element_type=jnp.float32)
             else:
-                buf[slot, k] = contract_rows(ins[slot, src], dy_ref[...])
+                buf[slot, k] = contract_rows(gat[0, :, cs], dy_ref[...])
             out_copy(b, k).start()
-
-            @pl.when(b + W_SLOTS < n_blocks)
-            def _():
-                in_copy(b + W_SLOTS, src).start()
         return carry
 
     lax.fori_loop(0, n_blocks, block, 0)
-    for d in small_in:
-        d.wait()
-    for d in small_out:
+    small = [pltpu.make_async_copy(src, dst, ssem.at[k])
+             for k, (src, dst) in enumerate(((y_in, y_hbm), (dx_in, dx_hbm), (dg_in, dg_hbm)))]
+    for d in small:
         d.start()
 
     def drain(b, carry):
@@ -474,7 +411,7 @@
         return carry
 
     lax.fori_loop(n_blocks - W_SLOTS, n_blocks, drain, 0)
-    for d in small_out:
+    for d in small:
         d.wait()
 
 
@@ -492,28 +429,28 @@
         f32, bf16 = jnp.float32, jnp.bfloat16
         anyspec = pl.BlockSpec(memory_space=pl.ANY)
         sem = pltpu.SemaphoreType.DMA
+        vm = pl.BlockSpec(memory_space=pltpu.VMEM)
         S = jax.ShapeDtypeStruct
         V = pltpu.VMEM
         small = [((rows, dl), bf16), ((rows, dl), bf16), ((1, dl), f32)]
         outs = pl.pallas_call(
             functools.partial(branch_kernel, d_model, n),
-            out_shape=[S((tok, fl), bf16)] * 3 + [S((tok, dl), bf16)] * 2 + [S(*s) for s in small],
+            out_shape=[V((3, tok, fl), bf16), V((dl, tok), bf16), V((tok, dl), bf16)] + [V(*s) for s in small],
             in_specs=[anyspec] * 6,
-            out_specs=[anyspec] * 8,
+            out_specs=[vm] * 6,
             scratch_shapes=[
-                V((rows, dl), bf16), V((1, dl), f32), V((tok, dl), bf16), V((tok, dl), bf16), *[V(*s) for s in small],
+                V((rows, dl), bf16), V((1, dl), f32), V((tok, dl), bf16),
                 V((dl, fl), bf16), V((dl, fl), bf16), V((fl, dl), bf16),
                 V((rows, dl), f32),
                 V((P_SLOTS, 2, rows, FC), f32), V((L_SLOTS, rows, FC), f32),
                 V((P_SLOTS, 2, rows // 2, FC), f32), V((L_SLOTS, rows // 2, FC), f32),
                 V((2 * n, 2, 3, rows // 4, half), f32), V((2 * n, 2, 3, rows // 8, half), f32),
-                V((3, tok, fl), bf16),
                 V((2, 2, rows, dl), f32), V((2, rows, dl), f32),
                 V((8, 8, 128), f32), V((8, 8, 128), f32), V((8, dl), f32), V((8, dl), f32),
                 sem((3, n)), sem((3,)), sem((4,)), sem((4,)), sem((8,)), sem((8,)), sem((8,)), sem((8,)),
                 sem((RING,)), sem((RING,)), sem((RING,)), sem((RING,)),
                 *[sem((2, RING)) for _ in range(10)],
-                sem((RING,)), sem((RING,)), sem((3, RING)), sem((5,)),
+                sem((RING,)), sem((RING,)),
             ],
             compiler_params=pltpu.CompilerParams(collective_id=0, has_side_effects=True, vmem_limit_bytes=VMEM_LIMIT),
             cost_estimate=pl.CostEstimate(flops=12 * tok * dl * fl, bytes_accessed=6 * dl * fl + 6 * tok * fl, transcendentals=0),
@@ -522,16 +459,14 @@
         dwg, dwu, dwd, y_blk, dx_blk, dg = pl.pallas_call(
             weight_grad_kernel,
             out_shape=[S((dl, fl), f32)] * 2 + [S((fl, dl), f32)] + [S(*s) for s in small],
-            in_specs=[anyspec] * 8,
+            in_specs=[vm] * 6,
             out_specs=[anyspec] * 6,
             scratch_shapes=[
-                V((tok, dl), bf16), V((tok, dl), bf16), V((dl, tok), bf16), *[V(*s) for s in small],
-                V((W_SLOTS, 3, tok, WB), bf16), V((W_SLOTS, 3, dl, WB), f32),
-                sem((W_SLOTS, 3)), sem((W_SLOTS, 3)), sem((8,)),
+                V((W_SLOTS, 3, dl, WB), f32), sem((W_SLOTS, 3)), sem((3,)),
             ],
             compiler_params=pltpu.CompilerParams(vmem_limit_bytes=VMEM_LIMIT),
             cost_estimate=pl.CostEstimate(flops=6 * tok * dl * fl, bytes_accessed=12 * dl * fl + 6 * tok * fl, transcendentals=0),
-        )(*outs)
+        )(*[pltpu.with_memory_space_constraint(o, pltpu.VMEM) for o in outs])
         return (y_blk, dx_blk, dwg, dwu, dwd, dg[0])
 
     return jax.shard_map(

time: 193 us -> 187 us (0.969)
  Pallas kernels: 192 us -> 186 us
    pallas_call x1, Pallas kernels: 21.1 us -> 16.4 us  [local_step(): pl.pallas_call(weight_grad_kernel, out_shape=[S((dl, fl), f32)] * 2 + [S(...]
where the time goes in v4:
time: 187 us
  Pallas kernels  186 us (99%)
    pallas_call x1, Pallas kernels, local_step(): pl.pallas_call(functools.partial(branch_kernel, d_model, n), out_shape=[V...  170 us
    pallas_call x1, Pallas kernels, local_step(): pl.pallas_call(weight_grad_kernel, out_shape=[S((dl, fl), f32)] * 2 + [S(...  16.4 us

profile of v4, /device:TPU:0, one launch (start us, length us, event | category | flops | bytes accessed | tf_op | source)
XLA Modules:
  0.0 186.9 jit_solution(9593011213319161623)
XLA Ops:
  0.6 169.8 %shard_map.109 = (bf16[3,256,8192]{2,1,0:T(8,128)(2,1)S(1)}, bf16[512,256]{1,0:T(8,128)(2,1)S(1)}, bf16[256,512]{1,0:T(8,128)(2,1)S(1)}, bf16[128,512]{1,0:T(8,1...) custom-call(bf16[128,512]{1,0:T(8,128)(2,1)} %x_hbm.1, bf16[128,512]{1,0:T(8,128)(2,1)} %dy_hbm.1, ...), custom_call_target="tpu_custom_call" | custom-call | flops 12884901888 | bytes 37748736 | tf_op jit(solution)/shard_map/pallas_call | solution.py:436
  170.5 16.4 %shard_map.110 = (f32[512,8192]{1,0:T(8,128)}, f32[512,8192]{1,0:T(8,128)}, f32[8192,512]{1,0:T(8,128)}, bf16[128,512]{1,0:T(8,128)(2,1)}, bf16[128,512]{1,0:T(8,128)(2,1)}, /*index=5*/f32[1,512]{1,0:T(1,128)}) custom-call(bf16[3,256,8192]{2,1,0:T(8,128)(2,1)S(1)} %get-tuple-element.18.gat, bf16[512,256]{1,0:T(8,128)(2,1)S(1)} %get-tuple-element.19.h_t, ...), custom_call_target="tpu_custom_call" | custom-call | flops 6442450944 | bytes 62914560 | tf_op jit(solution)/shard_map/pallas_call | solution.py:459

commit v5 on v4

--- a/solution.py
+++ b/solution.py
@@ -11,14 +11,15 @@
 MESH = pl.DeviceIdType.MESH
 FC = 512
 OWN_FIRST = 8
-LEAD = 6
+LEAD = 8
 P_SLOTS = 4
 L_SLOTS = LEAD + P_SLOTS
+HELD = 8
 RING = 16
 STAGES = (1, 3, 5, 7, 9, 10)
 WB = 512
 W_SLOTS = 3
-VMEM_LIMIT = 44 * 1024 * 1024
+VMEM_LIMIT = 48 * 1024 * 1024
 
 
 def contract_rows(left_op, right_op):
@@ -39,12 +40,13 @@
                   x_ref, gain_ref, h_ref,
                   wg, wu, wd, xh, part, part_d, dsum, dsum_d, r1, r2, acc, zin, st, rb, dgs, dgr,
                   wsem, isem, zs, zr, ss, sr, bs, br, ds, dr, dds, ddr, p1s, p1r, pds, pdr, p2s, p2r,
-                  g1s, g1r, g2s, g2r, gds, gdr):
+                  g1s, g1r, g2s, g2r, gds, gdr, a1s, a1r, a2s, a2r, ads, adr):
     half = FC // 2
     rows = x_ref.shape[0]
     q1, q2, q3 = rows // 2, rows // 4, rows // 8
     n_units = 2 * n_f
     last_oth = OWN_FIRST + n_f - 1
+    held = n_units - HELD
 
     ty = lax.axis_index("ty")
     t = lax.axis_index("tx")
@@ -181,20 +183,51 @@
     def p2_copy(j, r):
         return remote(r1.at[j, r, :, r_send[r], :], r2.at[j, r], p2s.at[r, ring(j)], p2r.at[r, ring(j)], dev2[r])
 
-    def g1_copy(j, r, off):
-        ref = gat.at[:, grows(j, off[r], q3), gcols(j, r)]
+    def g1_copy(j, r, off, lo):
+        ref = gat.at[lo:3, grows(j, off[r], q3), gcols(j, r)]
         return remote(ref, ref, g1s.at[r, ring(j)], g1r.at[r, ring(j)], dev2[r])
 
-    def g2_copy(j, r, off):
-        ref = gat.at[:, grows(j, off[r], q2), gcols(j, r)]
+    def g2_copy(j, r, off, lo):
+        ref = gat.at[lo:3, grows(j, off[r], q2), gcols(j, r)]
         return remote(ref, ref, g2s.at[r, ring(j)], g2r.at[r, ring(j)], dev1[r])
 
-    def gd_copy(j, off):
-        ref = gat.at[:, grows(j, off, q1), fcols(j)]
+    def gd_copy(j, off, lo):
+        ref = gat.at[lo:3, grows(j, off, q1), fcols(j)]
         return remote(ref, ref, gds.at[ring(j)], gdr.at[ring(j)], dev_c)
 
+    def a1_copy(k, r, off):
+        ref = gat.at[0, grows(held + k, off[r], q3), gcols(held + k, r)]
+        return remote(ref, ref, a1s.at[r, k], a1r.at[r, k], dev2[r])
+
+    def a2_copy(k, r, off):
+        ref = gat.at[0, grows(held + k, off[r], q2), gcols(held + k, r)]
+        return remote(ref, ref, a2s.at[r, k], a2r.at[r, k], dev1[r])
+
+    def ad_copy(k, off):
+        ref = gat.at[0, grows(held + k, off, q1), fcols(held + k)]
+        return remote(ref, ref, ads.at[k], adr.at[k], dev_c)
+
+    def by_arrays(j, body):
+        @pl.when(j < held)
+        def _():
+            body(0)
+
+        @pl.when(j >= held)
+        def _():
+            body(1)
+
+    def each_held(body):
+        def one(k, carry):
+            body(k)
+            return carry
+
+        lax.fori_loop(0, HELD, one, 0)
+
+    def da_dot(j):
+        part_d[lax.rem(j, L_SLOTS)] = contract_cols(dya_ref[trows(j), :], wd[fcols(j), :])
+
     def da_product(j):
-        part_d[lax.rem(j, L_SLOTS)] = contract_cols(dya_ref[trows(j), :], wd[fcols(j), :])
+        da_dot(j)
         dd_copy(j).start()
 
     def da_pair_sum(j):
@@ -204,20 +237,26 @@
         for r in range(2):
             pd_copy(j, r).start()
 
+    in_dy.wait()
+    wcopy(2, 0).wait()
+    da_dot(0)
+    pl.semaphore_wait(barrier, 8)
+    dd_copy(0).start()
     in_x.wait()
     x_own = x_ref[...].astype(jnp.float32)
     st[t] = pack_cols(jnp.sum(x_own, axis=1, keepdims=True), jnp.sum(x_own * x_own, axis=1, keepdims=True))
-    in_dy.wait()
-    in_gain.wait()
-    pl.semaphore_wait(barrier, 8)
     send_stats(st, ss, sr)
     zdy = remote(dya_ref.at[own, :], dya_ref.at[own, :], zs.at[0], zr.at[0], dev_z)
     zdy.start()
-    for i in range(LEAD):
+    for i in range(1, 3):
         wcopy(2, i).wait()
         da_product(i)
     for i in range(LEAD):
         da_pair_sum(i)
+        if i + 3 < LEAD:
+            wcopy(2, i + 3).wait()
+            da_product(i + 3)
+    in_gain.wait()
     acc[...] = jnp.zeros_like(acc)
 
     gain = gain_ref[...]
@@ -317,41 +356,69 @@
                 gat[0, rs, cs] = (swish * v).astype(jnp.bfloat16)
                 gat[1, rs, cs] = (da * v * sig * (1.0 + u * (1.0 - sig))).astype(jnp.bfloat16)
                 gat[2, rs, cs] = (da * swish).astype(jnp.bfloat16)
-                g1_copy(j, r, g_fin).start()
+            by_arrays(j, lambda lo: [g1_copy(j, r, g_fin, lo).start() for r in range(2)])
 
         @pl.when(jnp.logical_and(i >= STAGES[3], i < n_units + STAGES[3]))
         def _():
             j = i - STAGES[3]
-            for r in range(2):
-                g1_copy(j, r, g_fin_n).wait_recv()
-                g2_copy(j, r, g_keep1).start()
+
+            def forward(lo):
+                for r in range(2):
+                    g1_copy(j, r, g_fin_n, lo).wait_recv()
+                    g2_copy(j, r, g_keep1, lo).start()
+
+            by_arrays(j, forward)
 
         @pl.when(jnp.logical_and(i >= STAGES[4], i < n_units + STAGES[4]))
         def _():
             j = i - STAGES[4]
-            for r in range(2):
-                g2_copy(j, r, g_send1).wait_recv()
-            gd_copy(j, g_c[0]).start()
+
+            def to_core(lo):
+                for r in range(2):
+                    g2_copy(j, r, g_send1, lo).wait_recv()
+                gd_copy(j, g_c[0], lo).start()
+
+            by_arrays(j, to_core)
 
         @pl.when(i >= STAGES[5])
         def _():
             j = i - STAGES[5]
-            gd_copy(j, g_c[1]).wait_recv()
-
+            by_arrays(j, lambda lo: gd_copy(j, g_c[1], lo).wait_recv())
             cs = fcols(j)
             rs = trows(j)
             side = oth_of(j)
-            acc[side, 0] += jnp.dot(gat[0, rs, cs], wd[cs, :], preferred_element_type=jnp.float32)
+
+            @pl.when(j < held)
+            def _():
+                acc[side, 0] += jnp.dot(gat[0, rs, cs], wd[cs, :], preferred_element_type=jnp.float32)
+
             acc[side, 1] += contract_cols(gat[1, rs, cs], wg[:, cs]) + contract_cols(gat[2, rs, cs], wu[:, cs])
-            for r in range(2):
-                p2_copy(j, r).wait_send()
-                g1_copy(j, r, g_fin).wait_send()
-                g2_copy(j, r, g_keep1).wait_send()
-            gd_copy(j, g_c[0]).wait_send()
+
+            def sent(lo):
+                for r in range(2):
+                    p2_copy(j, r).wait_send()
+                    g1_copy(j, r, g_fin, lo).wait_send()
+                    g2_copy(j, r, g_keep1, lo).wait_send()
+                gd_copy(j, g_c[0], lo).wait_send()
+
+            by_arrays(j, sent)
 
             @pl.when(j == last_oth)
             def _():
                 z_sum.start()
+
+        @pl.when(i == n_units - 1 + STAGES[2])
+        def _():
+            each_held(lambda k: [a1_copy(k, r, g_fin).start() for r in range(2)])
+
+        @pl.when(i == n_units - 1 + STAGES[3])
+        def _():
+            def forward(k):
+                for r in range(2):
+                    a1_copy(k, r, g_fin_n).wait_recv()
+                    a2_copy(k, r, g_keep1).start()
+
+            each_held(forward)
         return carry
 
     lax.fori_loop(0, n_units + STAGES[5], step, 0)
@@ -364,6 +431,24 @@
     dgs[...] = jnp.broadcast_to(jnp.sum(d_hnorm * xh[...], axis=0, keepdims=True), dgs.shape)
     z_dg = remote(dgs, dgr, zs.at[3], zr.at[3], dev_z)
     z_dg.start()
+
+    def to_core(k):
+        for r in range(2):
+            a2_copy(k, r, g_send1).wait_recv()
+        ad_copy(k, g_c[0]).start()
+
+    each_held(to_core)
+
+    def m_product(k):
+        ad_copy(k, g_c[1]).wait_recv()
+        cs = fcols(held + k)
+        acc[0, 0] += jnp.dot(gat[0, own, cs], wd[cs, :], preferred_element_type=jnp.float32)
+        for r in range(2):
+            a1_copy(k, r, g_fin).wait_send()
+            a2_copy(k, r, g_keep1).wait_send()
+        ad_copy(k, g_c[0]).wait_send()
+
+    each_held(m_product)
     y_ref[...] = (x_ref[...].astype(jnp.float32) + (acc[0, 0] + zin[0])).astype(jnp.bfloat16)
     zdy.wait_send()
     h_copy(own).wait_send()
@@ -451,6 +536,7 @@
                 sem((RING,)), sem((RING,)), sem((RING,)), sem((RING,)),
                 *[sem((2, RING)) for _ in range(10)],
                 sem((RING,)), sem((RING,)),
+                *[sem((2, HELD)) for _ in range(4)], sem((HELD,)), sem((HELD,)),
             ],
             compiler_params=pltpu.CompilerParams(collective_id=0, has_side_effects=True, vmem_limit_bytes=VMEM_LIMIT),
             cost_estimate=pl.CostEstimate(flops=12 * tok * dl * fl, bytes_accessed=6 * dl * fl + 6 * tok * fl, transcendentals=0),

time: 187 us -> 185 us (0.989)
  Pallas kernels: 186 us -> 184 us
where the time goes in v5:
time: 185 us
  Pallas kernels  184 us (99%)
    pallas_call x1, Pallas kernels, local_step(): pl.pallas_call(functools.partial(branch_kernel, d_model, n), out_shape=[V...  168 us
    pallas_call x1, Pallas kernels, local_step(): pl.pallas_call(weight_grad_kernel, out_shape=[S((dl, fl), f32)] * 2 + [S(...  16.4 us

profile of v5, /device:TPU:0, one launch (start us, length us, event | category | flops | bytes accessed | tf_op | source)
XLA Modules:
  0.0 185.0 jit_solution(7530139118445073416)
XLA Ops:
  0.6 168.0 %shard_map.109 = (bf16[3,256,8192]{2,1,0:T(8,128)(2,1)S(1)}, bf16[512,256]{1,0:T(8,128)(2,1)S(1)}, bf16[256,512]{1,0:T(8,128)(2,1)S(1)}, bf16[128,512]{1,0:T(8,1...) custom-call(bf16[128,512]{1,0:T(8,128)(2,1)} %x_hbm.1, bf16[128,512]{1,0:T(8,128)(2,1)} %dy_hbm.1, ...), custom_call_target="tpu_custom_call" | custom-call | flops 12884901888 | bytes 37748736 | tf_op jit(solution)/shard_map/pallas_call | solution.py:521
  168.6 16.4 %shard_map.110 = (f32[512,8192]{1,0:T(8,128)}, f32[512,8192]{1,0:T(8,128)}, f32[8192,512]{1,0:T(8,128)}, bf16[128,512]{1,0:T(8,128)(2,1)}, bf16[128,512]{1,0:T(8,128)(2,1)}, /*index=5*/f32[1,512]{1,0:T(1,128)}) custom-call(bf16[3,256,8192]{2,1,0:T(8,128)(2,1)S(1)} %get-tuple-element.18.gat, bf16[512,256]{1,0:T(8,128)(2,1)S(1)} %get-tuple-element.19.h_t, ...), custom_call_target="tpu_custom_call" | custom-call | flops 6442450944 | bytes 62914560 | tf_op jit(solution)/shard_map/pallas_call | solution.py:545

commit v6 on v5

--- a/solution.py
+++ b/solution.py
@@ -9,14 +9,14 @@
 
 LN_EPS = 1e-6
 MESH = pl.DeviceIdType.MESH
-FC = 512
-OWN_FIRST = 8
-LEAD = 8
-P_SLOTS = 4
+FC = 256
+OWN_FIRST = 16
+LEAD = 14
+P_SLOTS = 6
 L_SLOTS = LEAD + P_SLOTS
-HELD = 8
-RING = 16
-STAGES = (1, 3, 5, 7, 9, 10)
+HELD = 16
+RING = 24
+STAGES = (1, 4, 7, 10, 13, 14)
 WB = 512
 W_SLOTS = 3
 VMEM_LIMIT = 48 * 1024 * 1024

time: 185 us -> 192 us (1.038)
  Pallas kernels: 184 us -> 192 us
    pallas_call x1, Pallas kernels: 168 us -> 175 us  [local_step(): pl.pallas_call(functools.partial(branch_kernel, d_model, n), out_shape=[V...]
where the time goes in v6:
time: 192 us
  Pallas kernels  192 us (100%)
    pallas_call x1, Pallas kernels, local_step(): pl.pallas_call(functools.partial(branch_kernel, d_model, n), out_shape=[V...  175 us
    pallas_call x1, Pallas kernels, local_step(): pl.pallas_call(weight_grad_kernel, out_shape=[S((dl, fl), f32)] * 2 + [S(...  16.4 us

profile of v6, /device:TPU:0, one launch (start us, length us, event | category | flops | bytes accessed | tf_op | source)
XLA Modules:
  0.0 192.4 jit_solution(4756156684762278196)
XLA Ops:
  0.6 175.3 %shard_map.109 = (bf16[3,256,8192]{2,1,0:T(8,128)(2,1)S(1)}, bf16[512,256]{1,0:T(8,128)(2,1)S(1)}, bf16[256,512]{1,0:T(8,128)(2,1)S(1)}, bf16[128,512]{1,0:T(8,1...) custom-call(bf16[128,512]{1,0:T(8,128)(2,1)} %x_hbm.1, bf16[128,512]{1,0:T(8,128)(2,1)} %dy_hbm.1, ...), custom_call_target="tpu_custom_call" | custom-call | flops 12884901888 | bytes 37748736 | tf_op jit(solution)/shard_map/pallas_call | solution.py:521
  176.0 16.4 %shard_map.110 = (f32[512,8192]{1,0:T(8,128)}, f32[512,8192]{1,0:T(8,128)}, f32[8192,512]{1,0:T(8,128)}, bf16[128,512]{1,0:T(8,128)(2,1)}, bf16[128,512]{1,0:T(8,128)(2,1)}, /*index=5*/f32[1,512]{1,0:T(1,128)}) custom-call(bf16[3,256,8192]{2,1,0:T(8,128)(2,1)S(1)} %get-tuple-element.18.gat, bf16[512,256]{1,0:T(8,128)(2,1)S(1)} %get-tuple-element.19.h_t, ...), custom_call_target="tpu_custom_call" | custom-call | flops 6442450944 | bytes 62914560 | tf_op jit(solution)/shard_map/pallas_call | solution.py:545

commit v7 on v5

--- a/solution.py
+++ b/solution.py
@@ -17,7 +17,6 @@
 HELD = 8
 RING = 16
 STAGES = (1, 3, 5, 7, 9, 10)
-WB = 512
 W_SLOTS = 3
 VMEM_LIMIT = 48 * 1024 * 1024
 
@@ -77,6 +76,9 @@
     def fcols(j):
         return pl.ds(mo(f_of(j) * FC, FC), FC)
 
+    def rcols(j, r):
+        return pl.ds(mo(f_of(j) * FC + r * half, half), half)
+
     def trows(j):
         return pl.ds(mo(base_of(j), rows), rows)
 
@@ -147,7 +149,7 @@
     send1 = (seg(c * q1 + (1 - xc) * q2, q2), seg(c * q1 + (1 - yc) * q2, q2))
     r_keep = (seg(yc * q3, q3), seg(xc * q3, q3))
     r_send = (seg((1 - yc) * q3, q3), seg((1 - xc) * q3, q3))
-    colw = (slice(0, half), slice(half, FC))
+    lanes = [slice(k * half, (k + 1) * half) for k in range(3)]
     dev1, dev2 = (dev_x, dev_y), (dev_y, dev_x)
     g_c = (c * q1, (1 - c) * q1)
     g_keep1 = (c * q1 + xc * q2, c * q1 + yc * q2)
@@ -155,9 +157,6 @@
     g_fin = (g_keep1[0] + yc * q3, g_keep1[1] + xc * q3)
     g_fin_n = (g_keep1[0] + (1 - yc) * q3, g_keep1[1] + (1 - xc) * q3)
 
-    def gcols(j, r):
-        return pl.ds(mo(f_of(j) * FC + r * half, half), half)
-
     def grows(j, off, size):
         return pl.ds(mo(base_of(j) + off, size), size)
 
@@ -166,45 +165,45 @@
 
     def d_copy(j):
         slot = lax.rem(j, P_SLOTS)
-        return remote(part.at[slot, :, oth_c, :], dsum.at[slot], ds.at[ring(j)], dr.at[ring(j)], dev_c)
+        return remote(part.at[slot, :, :, oth_c, :], dsum.at[slot], ds.at[ring(j)], dr.at[ring(j)], dev_c)
 
     def dd_copy(j):
         slot = lax.rem(j, L_SLOTS)
-        return remote(part_d.at[slot, oth_c, :], dsum_d.at[slot], dds.at[ring(j)], ddr.at[ring(j)], dev_c)
+        return remote(part_d.at[slot, :, oth_c, :], dsum_d.at[slot], dds.at[ring(j)], ddr.at[ring(j)], dev_c)
 
     def p1_copy(j, r):
-        return remote(part.at[lax.rem(j, P_SLOTS), :, send1[r], colw[r]], r1.at[j, r, 0:2],
+        return remote(part.at[lax.rem(j, P_SLOTS), r, :, send1[r], :], r1.at[j, r, 0:2],
                       p1s.at[r, ring(j)], p1r.at[r, ring(j)], dev1[r])
 
     def pd_copy(j, r):
-        return remote(part_d.at[lax.rem(j, L_SLOTS), send1[r], colw[r]], r1.at[j, r, 2],
+        return remote(part_d.at[lax.rem(j, L_SLOTS), r, send1[r], :], r1.at[j, r, 2],
                       pds.at[r, ring(j)], pdr.at[r, ring(j)], dev1[r])
 
     def p2_copy(j, r):
         return remote(r1.at[j, r, :, r_send[r], :], r2.at[j, r], p2s.at[r, ring(j)], p2r.at[r, ring(j)], dev2[r])
 
     def g1_copy(j, r, off, lo):
-        ref = gat.at[lo:3, grows(j, off[r], q3), gcols(j, r)]
+        ref = gat.at[f_of(j), r, grows(j, off[r], q3), lo * half:]
         return remote(ref, ref, g1s.at[r, ring(j)], g1r.at[r, ring(j)], dev2[r])
 
     def g2_copy(j, r, off, lo):
-        ref = gat.at[lo:3, grows(j, off[r], q2), gcols(j, r)]
+        ref = gat.at[f_of(j), r, grows(j, off[r], q2), lo * half:]
         return remote(ref, ref, g2s.at[r, ring(j)], g2r.at[r, ring(j)], dev1[r])
 
     def gd_copy(j, off, lo):
-        ref = gat.at[lo:3, grows(j, off, q1), fcols(j)]
+        ref = gat.at[f_of(j), :, grows(j, off, q1), lo * half:]
         return remote(ref, ref, gds.at[ring(j)], gdr.at[ring(j)], dev_c)
 
     def a1_copy(k, r, off):
-        ref = gat.at[0, grows(held + k, off[r], q3), gcols(held + k, r)]
+        ref = gat.at[f_of(held + k), r, grows(held + k, off[r], q3), lanes[0]]
         return remote(ref, ref, a1s.at[r, k], a1r.at[r, k], dev2[r])
 
     def a2_copy(k, r, off):
-        ref = gat.at[0, grows(held + k, off[r], q2), gcols(held + k, r)]
+        ref = gat.at[f_of(held + k), r, grows(held + k, off[r], q2), lanes[0]]
         return remote(ref, ref, a2s.at[r, k], a2r.at[r, k], dev1[r])
 
     def ad_copy(k, off):
-        ref = gat.at[0, grows(held + k, off, q1), fcols(held + k)]
+        ref = gat.at[f_of(held + k), :, grows(held + k, off, q1), lanes[0]]
         return remote(ref, ref, ads.at[k], adr.at[k], dev_c)
 
     def by_arrays(j, body):
@@ -224,7 +223,8 @@
         lax.fori_loop(0, HELD, one, 0)
 
     def da_dot(j):
-        part_d[lax.rem(j, L_SLOTS)] = contract_cols(dya_ref[trows(j), :], wd[fcols(j), :])
+        for r in range(2):
+            part_d[lax.rem(j, L_SLOTS), r] = contract_cols(dya_ref[trows(j), :], wd[rcols(j, r), :])
 
     def da_product(j):
         da_dot(j)
@@ -233,8 +233,8 @@
     def da_pair_sum(j):
         dd_copy(j).wait_recv()
         slot = lax.rem(j, L_SLOTS)
-        part_d[slot, own_c, :] = part_d[slot, own_c, :] + dsum_d[slot]
         for r in range(2):
+            part_d[slot, r, own_c, :] = part_d[slot, r, own_c, :] + dsum_d[slot, r]
             pd_copy(j, r).start()
 
     in_dy.wait()
@@ -272,6 +272,9 @@
 
     h_copy(own).start()
 
+    def m_part(f, rs, j):
+        return sum(jnp.dot(gat[f, r, rs, lanes[0]], wd[rcols(j, r), :], preferred_element_type=jnp.float32) for r in range(2))
+
     z_sum = remote(acc.at[1], zin, zs.at[2], zr.at[2], dev_z)
 
     def step(i, carry):
@@ -304,11 +307,11 @@
 
         @pl.when(i < n_units)
         def _():
-            cs = fcols(i)
             slot = lax.rem(i, P_SLOTS)
             h = h_ref[trows(i), :]
-            part[slot, 0] = jnp.dot(h, wg[:, cs], preferred_element_type=jnp.float32)
-            part[slot, 1] = jnp.dot(h, wu[:, cs], preferred_element_type=jnp.float32)
+            for r in range(2):
+                part[slot, r, 0] = jnp.dot(h, wg[:, rcols(i, r)], preferred_element_type=jnp.float32)
+                part[slot, r, 1] = jnp.dot(h, wu[:, rcols(i, r)], preferred_element_type=jnp.float32)
             d_copy(i).start()
 
         @pl.when(i + LEAD < n_units)
@@ -320,9 +323,9 @@
             j = i - STAGES[0]
             d_copy(j).wait_recv()
             slot = lax.rem(j, P_SLOTS)
-            for k in range(2):
-                part[slot, k, own_c, :] = part[slot, k, own_c, :] + dsum[slot, k]
             for r in range(2):
+                for k in range(2):
+                    part[slot, r, k, own_c, :] = part[slot, r, k, own_c, :] + dsum[slot, r, k]
                 p1_copy(j, r).start()
 
             @pl.when(j + LEAD < n_units)
@@ -337,8 +340,8 @@
                 pd_copy(j, r).wait_recv()
                 p1_copy(j, r).wait_recv()
                 for k in range(2):
-                    r1[j, r, k] = r1[j, r, k] + part[slot, k, keep1[r], colw[r]]
-                r1[j, r, 2] = r1[j, r, 2] + part_d[lax.rem(j, L_SLOTS), keep1[r], colw[r]]
+                    r1[j, r, k] = r1[j, r, k] + part[slot, r, k, keep1[r], :]
+                r1[j, r, 2] = r1[j, r, 2] + part_d[lax.rem(j, L_SLOTS), r, keep1[r], :]
                 p2_copy(j, r).start()
 
         @pl.when(jnp.logical_and(i >= STAGES[2], i < n_units + STAGES[2]))
@@ -351,11 +354,11 @@
                 da = r1[j, r, 2, r_keep[r], :] + r2[j, r, 2]
                 sig = jax.nn.sigmoid(u)
                 swish = u * sig
-                cs = gcols(j, r)
+                f = f_of(j)
                 rs = grows(j, g_fin[r], q3)
-                gat[0, rs, cs] = (swish * v).astype(jnp.bfloat16)
-                gat[1, rs, cs] = (da * v * sig * (1.0 + u * (1.0 - sig))).astype(jnp.bfloat16)
-                gat[2, rs, cs] = (da * swish).astype(jnp.bfloat16)
+                gat[f, r, rs, lanes[0]] = (swish * v).astype(jnp.bfloat16)
+                gat[f, r, rs, lanes[1]] = (da * v * sig * (1.0 + u * (1.0 - sig))).astype(jnp.bfloat16)
+                gat[f, r, rs, lanes[2]] = (da * swish).astype(jnp.bfloat16)
             by_arrays(j, lambda lo: [g1_copy(j, r, g_fin, lo).start() for r in range(2)])
 
         @pl.when(jnp.logical_and(i >= STAGES[3], i < n_units + STAGES[3]))
@@ -384,15 +387,16 @@
         def _():
             j = i - STAGES[5]
             by_arrays(j, lambda lo: gd_copy(j, g_c[1], lo).wait_recv())
-            cs = fcols(j)
+            f = f_of(j)
             rs = trows(j)
             side = oth_of(j)
 
             @pl.when(j < held)
             def _():
-                acc[side, 0] += jnp.dot(gat[0, rs, cs], wd[cs, :], preferred_element_type=jnp.float32)
-
-            acc[side, 1] += contract_cols(gat[1, rs, cs], wg[:, cs]) + contract_cols(gat[2, rs, cs], wu[:, cs])
+                acc[side, 0] += m_part(f, rs, j)
+
+            acc[side, 1] += sum(contract_cols(gat[f, r, rs, lanes[1]], wg[:, rcols(j, r)])
+                                + contract_cols(gat[f, r, rs, lanes[2]], wu[:, rcols(j, r)]) for r in range(2))
 
             def sent(lo):
                 for r in range(2):
@@ -441,8 +445,7 @@
 
     def m_product(k):
         ad_copy(k, g_c[1]).wait_recv()
-        cs = fcols(held + k)
-        acc[0, 0] += jnp.dot(gat[0, own, cs], wd[cs, :], preferred_element_type=jnp.float32)
+        acc[0, 0] += m_part(f_of(held + k), own, held + k)
         for r in range(2):
             a1_copy(k, r, g_fin).wait_send()
             a2_copy(k, r, g_keep1).wait_send()
@@ -461,7 +464,9 @@
 
 def weight_grad_kernel(gat, h_t, dy_ref, y_in, dx_in, dg_in,
                        dwg_hbm, dwu_hbm, dwd_hbm, y_hbm, dx_hbm, dg_hbm, buf, bsem, ssem):
-    n_blocks = gat.shape[2] // WB
+    n_blocks, _, _, width = gat.shape
+    half = width // 3
+    WB = 2 * half
 
     def out_copy(b, k):
         cs = pl.ds(mo(b * WB, WB), WB)
@@ -470,17 +475,19 @@
         return pltpu.make_async_copy(buf.at[slot, k], dst, bsem.at[slot, k])
 
     def block(b, carry):
-        cs = pl.ds(mo(b * WB, WB), WB)
         slot = lax.rem(b, W_SLOTS)
         for k in range(3):
             @pl.when(b >= W_SLOTS)
             def _():
                 out_copy(b - W_SLOTS, k).wait()
 
-            if k < 2:
-                buf[slot, k] = jnp.dot(h_t[...], gat[k + 1, :, cs], preferred_element_type=jnp.float32)
-            else:
-                buf[slot, k] = contract_rows(gat[0, :, cs], dy_ref[...])
+            for r in range(2):
+                rs = slice(r * half, (r + 1) * half)
+                src = gat[b, r, :, (k + 1) % 3 * half:((k + 1) % 3 + 1) * half]
+                if k < 2:
+                    buf[slot, k, :, rs] = jnp.dot(h_t[...], src, preferred_element_type=jnp.float32)
+                else:
+                    buf[slot, k, rs, :] = contract_rows(src, dy_ref[...])
             out_copy(b, k).start()
         return carry
 
@@ -520,15 +527,15 @@
         small = [((rows, dl), bf16), ((rows, dl), bf16), ((1, dl), f32)]
         outs = pl.pallas_call(
             functools.partial(branch_kernel, d_model, n),
-            out_shape=[V((3, tok, fl), bf16), V((dl, tok), bf16), V((tok, dl), bf16)] + [V(*s) for s in small],
+            out_shape=[V((n, 2, tok, 3 * half), bf16), V((dl, tok), bf16), V((tok, dl), bf16)] + [V(*s) for s in small],
             in_specs=[anyspec] * 6,
             out_specs=[vm] * 6,
             scratch_shapes=[
                 V((rows, dl), bf16), V((1, dl), f32), V((tok, dl), bf16),
                 V((dl, fl), bf16), V((dl, fl), bf16), V((fl, dl), bf16),
                 V((rows, dl), f32),
-                V((P_SLOTS, 2, rows, FC), f32), V((L_SLOTS, rows, FC), f32),
-                V((P_SLOTS, 2, rows // 2, FC), f32), V((L_SLOTS, rows // 2, FC), f32),
+                V((P_SLOTS, 2, 2, rows, half), f32), V((L_SLOTS, 2, rows, half), f32),
+                V((P_SLOTS, 2, 2, rows // 2, half), f32), V((L_SLOTS, 2, rows // 2, half), f32),
                 V((2 * n, 2, 3, rows // 4, half), f32), V((2 * n, 2, 3, rows // 8, half), f32),
                 V((2, 2, rows, dl), f32), V((2, rows, dl), f32),
                 V((8, 8, 128), f32), V((8, 8, 128), f32), V((8, dl), f32), V((8, dl), f32),
@@ -548,7 +555,7 @@
             in_specs=[vm] * 6,
             out_specs=[anyspec] * 6,
             scratch_shapes=[
-                V((W_SLOTS, 3, dl, WB), f32), sem((W_SLOTS, 3)), sem((3,)),
+                V((W_SLOTS, 3, dl, FC), f32), sem((W_SLOTS, 3)), sem((3,)),
             ],
             compiler_params=pltpu.CompilerParams(vmem_limit_bytes=VMEM_LIMIT),
             cost_estimate=pl.CostEstimate(flops=6 * tok * dl * fl, bytes_accessed=12 * dl * fl + 6 * tok * fl, transcendentals=0),

time: 185 us -> 185 us (level)
  no operation moved by 1% of the time
where the time goes in v7:
time: 185 us
  Pallas kernels  184 us (99%)
    pallas_call x1, Pallas kernels, local_step(): pl.pallas_call(functools.partial(branch_kernel, d_model, n), out_shape=[V...  168 us
    pallas_call x1, Pallas kernels, local_step(): pl.pallas_call(weight_grad_kernel, out_shape=[S((dl, fl), f32)] * 2 + [S(...  16.4 us

profile of v7, /device:TPU:0, one launch (start us, length us, event | category | flops | bytes accessed | tf_op | source)
XLA Modules:
  0.0 185.1 jit_solution(17778110350201238377)
XLA Ops:
  0.6 168.0 %shard_map.109 = (bf16[16,2,256,768]{3,2,1,0:T(8,128)(2,1)S(1)}, bf16[512,256]{1,0:T(8,128)(2,1)S(1)}, bf16[256,512]{1,0:T(8,128)(2,1)S(1)}, bf16[128,512]{1,0:T...) custom-call(bf16[128,512]{1,0:T(8,128)(2,1)} %x_hbm.1, bf16[128,512]{1,0:T(8,128)(2,1)} %dy_hbm.1, ...), custom_call_target="tpu_custom_call" | custom-call | flops 12884901888 | bytes 37748736 | tf_op jit(solution)/shard_map/pallas_call | solution.py:528
  168.6 16.4 %shard_map.110 = (f32[512,8192]{1,0:T(8,128)}, f32[512,8192]{1,0:T(8,128)}, f32[8192,512]{1,0:T(8,128)}, bf16[128,512]{1,0:T(8,128)(2,1)}, bf16[128,512]{1,0:T(8,128)(2,1)}, /*index=5*/f32[1,512]{1,0:T(1,128)}) custom-call(bf16[16,2,256,768]{3,2,1,0:T(8,128)(2,1)S(1)} %get-tuple-element.18.gat, bf16[512,256]{1,0:T(8,128)(2,1)S(1)} %get-tuple-element.19.h_t, ...), custom_call_target="tpu_custom_call" | custom-call | flops 6442450944 | bytes 62914560 | tf_op jit(solution)/shard_map/pallas_call | solution.py:552

commit v8 on v7

--- a/solution.py
+++ b/solution.py
@@ -9,16 +9,17 @@
 
 LN_EPS = 1e-6
 MESH = pl.DeviceIdType.MESH
-FC = 512
-OWN_FIRST = 8
-LEAD = 8
-P_SLOTS = 4
+FC = 1024
+OWN_FIRST = 4
+LEAD = 4
+P_SLOTS = 3
+D_SLOTS = 4
 L_SLOTS = LEAD + P_SLOTS
-HELD = 8
+HELD = 4
 RING = 16
-STAGES = (1, 3, 5, 7, 9, 10)
+STAGES = (1, 2, 4, 6, 8, 9)
 W_SLOTS = 3
-VMEM_LIMIT = 48 * 1024 * 1024
+VMEM_LIMIT = 49 * 1024 * 1024
 
 
 def contract_rows(left_op, right_op):
@@ -165,7 +166,7 @@
 
     def d_copy(j):
         slot = lax.rem(j, P_SLOTS)
-        return remote(part.at[slot, :, :, oth_c, :], dsum.at[slot], ds.at[ring(j)], dr.at[ring(j)], dev_c)
+        return remote(part.at[slot, :, :, oth_c, :], dsum.at[lax.rem(j, D_SLOTS)], ds.at[ring(j)], dr.at[ring(j)], dev_c)
 
     def dd_copy(j):
         slot = lax.rem(j, L_SLOTS)
@@ -325,7 +326,7 @@
             slot = lax.rem(j, P_SLOTS)
             for r in range(2):
                 for k in range(2):
-                    part[slot, r, k, own_c, :] = part[slot, r, k, own_c, :] + dsum[slot, r, k]
+                    part[slot, r, k, own_c, :] = part[slot, r, k, own_c, :] + dsum[lax.rem(j, D_SLOTS), r, k]
                 p1_copy(j, r).start()
 
             @pl.when(j + LEAD < n_units)
@@ -463,16 +464,17 @@
 
 
 def weight_grad_kernel(gat, h_t, dy_ref, y_in, dx_in, dg_in,
-                       dwg_hbm, dwu_hbm, dwd_hbm, y_hbm, dx_hbm, dg_hbm, buf, bsem, ssem):
-    n_blocks, _, _, width = gat.shape
-    half = width // 3
-    WB = 2 * half
+                       dwg_hbm, dwu_hbm, dwd_hbm, y_hbm, dx_hbm, dg_hbm, buf, buf2, bsem, ssem):
+    n_f, _, _, width = gat.shape
+    n_blocks = 2 * n_f
+    wb = width // 3
 
     def out_copy(b, k):
-        cs = pl.ds(mo(b * WB, WB), WB)
+        cs = pl.ds(mo(b * wb, wb), wb)
         dst = (dwg_hbm.at[:, cs], dwu_hbm.at[:, cs], dwd_hbm.at[cs, :])[k]
         slot = lax.rem(b, W_SLOTS)
-        return pltpu.make_async_copy(buf.at[slot, k], dst, bsem.at[slot, k])
+        src = buf.at[slot, k] if k < 2 else buf2.at[slot]
+        return pltpu.make_async_copy(src, dst, bsem.at[slot, k])
 
     def block(b, carry):
         slot = lax.rem(b, W_SLOTS)
@@ -481,13 +483,11 @@
             def _():
                 out_copy(b - W_SLOTS, k).wait()
 
-            for r in range(2):
-                rs = slice(r * half, (r + 1) * half)
-                src = gat[b, r, :, (k + 1) % 3 * half:((k + 1) % 3 + 1) * half]
-                if k < 2:
-                    buf[slot, k, :, rs] = jnp.dot(h_t[...], src, preferred_element_type=jnp.float32)
-                else:
-                    buf[slot, k, rs, :] = contract_rows(src, dy_ref[...])
+            src = gat[lax.div(b, 2), lax.rem(b, 2), :, (k + 1) % 3 * wb:((k + 1) % 3 + 1) * wb]
+            if k < 2:
+                buf[slot, k] = jnp.dot(h_t[...], src, preferred_element_type=jnp.float32)
+            else:
+                buf2[slot] = contract_rows(src, dy_ref[...])
             out_copy(b, k).start()
         return carry
 
@@ -535,7 +535,7 @@
                 V((dl, fl), bf16), V((dl, fl), bf16), V((fl, dl), bf16),
                 V((rows, dl), f32),
                 V((P_SLOTS, 2, 2, rows, half), f32), V((L_SLOTS, 2, rows, half), f32),
-                V((P_SLOTS, 2, 2, rows // 2, half), f32), V((L_SLOTS, 2, rows // 2, half), f32),
+                V((D_SLOTS, 2, 2, rows // 2, half), f32), V((L_SLOTS, 2, rows // 2, half), f32),
                 V((2 * n, 2, 3, rows // 4, half), f32), V((2 * n, 2, 3, rows // 8, half), f32),
                 V((2, 2, rows, dl), f32), V((2, rows, dl), f32),
                 V((8, 8, 128), f32), V((8, 8, 128), f32), V((8, dl), f32), V((8, dl), f32),
@@ -555,7 +555,7 @@
             in_specs=[vm] * 6,
             out_specs=[anyspec] * 6,
             scratch_shapes=[
-                V((W_SLOTS, 3, dl, FC), f32), sem((W_SLOTS, 3)), sem((3,)),
+                V((W_SLOTS, 2, dl, half), f32), V((W_SLOTS, half, dl), f32), sem((W_SLOTS, 3)), sem((3,)),
             ],
             compiler_params=pltpu.CompilerParams(vmem_limit_bytes=VMEM_LIMIT),
             cost_estimate=pl.CostEstimate(flops=6 * tok * dl * fl, bytes_accessed=12 * dl * fl + 6 * tok * fl, transcendentals=0),

time: 185 us -> 190 us (1.027)
  Pallas kernels: 184 us -> 190 us
    pallas_call x1, Pallas kernels: 168 us -> 173 us  [local_step(): pl.pallas_call(functools.partial(branch_kernel, d_model, n), out_shape=[V...]
where the time goes in v8:
time: 190 us
  Pallas kernels  190 us (100%)
    pallas_call x1, Pallas kernels, local_step(): pl.pallas_call(functools.partial(branch_kernel, d_model, n), out_shape=[V...  173 us
    pallas_call x1, Pallas kernels, local_step(): pl.pallas_call(weight_grad_kernel, out_shape=[S((dl, fl), f32)] * 2 + [S(...  16.4 us

profile of v8, /device:TPU:0, one launch (start us, length us, event | category | flops | bytes accessed | tf_op | source)
XLA Modules:
  0.0 190.3 jit_solution(6119539342482575051)
XLA Ops:
  0.6 173.2 %shard_map.109 = (bf16[8,2,256,1536]{3,2,1,0:T(8,128)(2,1)S(1)}, bf16[512,256]{1,0:T(8,128)(2,1)S(1)}, bf16[256,512]{1,0:T(8,128)(2,1)S(1)}, bf16[128,512]{1,0:T...) custom-call(bf16[128,512]{1,0:T(8,128)(2,1)} %x_hbm.1, bf16[128,512]{1,0:T(8,128)(2,1)} %dy_hbm.1, ...), custom_call_target="tpu_custom_call" | custom-call | flops 12884901888 | bytes 37748736 | tf_op jit(solution)/shard_map/pallas_call | solution.py:528
  173.9 16.4 %shard_map.110 = (f32[512,8192]{1,0:T(8,128)}, f32[512,8192]{1,0:T(8,128)}, f32[8192,512]{1,0:T(8,128)}, bf16[128,512]{1,0:T(8,128)(2,1)}, bf16[128,512]{1,0:T(8,128)(2,1)}, /*index=5*/f32[1,512]{1,0:T(1,128)}) custom-call(bf16[8,2,256,1536]{3,2,1,0:T(8,128)(2,1)S(1)} %get-tuple-element.18.gat, bf16[512,256]{1,0:T(8,128)(2,1)S(1)} %get-tuple-element.19.h_t, ...), custom_call_target="tpu_custom_call" | custom-call | flops 6442450944 | bytes 62914560 | tf_op jit(solution)/shard_map/pallas_call | solution.py:552

commit v9 on v7

--- a/solution.py
+++ b/solution.py
@@ -16,7 +16,7 @@
 L_SLOTS = LEAD + P_SLOTS
 HELD = 8
 RING = 16
-STAGES = (1, 3, 5, 7, 9, 10)
+STAGES = (1, 3, 6, 9, 13, 14)
 W_SLOTS = 3
 VMEM_LIMIT = 48 * 1024 * 1024
 

time: 185 us -> 190 us (1.027)
  Pallas kernels: 184 us -> 189 us
    pallas_call x1, Pallas kernels: 168 us -> 172 us  [local_step(): pl.pallas_call(functools.partial(branch_kernel, d_model, n), out_shape=[V...]
where the time goes in v9:
time: 190 us; the launch traced here: 189 us
  Pallas kernels  189 us (99%)
    pallas_call x1, Pallas kernels, local_step(): pl.pallas_call(functools.partial(branch_kernel, d_model, n), out_shape=[V...  172 us
    pallas_call x1, Pallas kernels, local_step(): pl.pallas_call(weight_grad_kernel, out_shape=[S((dl, fl), f32)] * 2 + [S(...  16.4 us

profile of v9, /device:TPU:0, one launch (start us, length us, event | category | flops | bytes accessed | tf_op | source)
XLA Modules:
  0.0 189.4 jit_solution(17717527922119159886)
XLA Ops:
  0.6 172.4 %shard_map.109 = (bf16[16,2,256,768]{3,2,1,0:T(8,128)(2,1)S(1)}, bf16[512,256]{1,0:T(8,128)(2,1)S(1)}, bf16[256,512]{1,0:T(8,128)(2,1)S(1)}, bf16[128,512]{1,0:T...) custom-call(bf16[128,512]{1,0:T(8,128)(2,1)} %x_hbm.1, bf16[128,512]{1,0:T(8,128)(2,1)} %dy_hbm.1, ...), custom_call_target="tpu_custom_call" | custom-call | flops 12884901888 | bytes 37748736 | tf_op jit(solution)/shard_map/pallas_call | solution.py:528
  173.0 16.4 %shard_map.110 = (f32[512,8192]{1,0:T(8,128)}, f32[512,8192]{1,0:T(8,128)}, f32[8192,512]{1,0:T(8,128)}, bf16[128,512]{1,0:T(8,128)(2,1)}, bf16[128,512]{1,0:T(8,128)(2,1)}, /*index=5*/f32[1,512]{1,0:T(1,128)}) custom-call(bf16[16,2,256,768]{3,2,1,0:T(8,128)(2,1)S(1)} %get-tuple-element.18.gat, bf16[512,256]{1,0:T(8,128)(2,1)S(1)} %get-tuple-element.19.h_t, ...), custom_call_target="tpu_custom_call" | custom-call | flops 6442450944 | bytes 62914560 | tf_op jit(solution)/shard_map/pallas_call | solution.py:552

commit v10 on v8

--- a/solution.py
+++ b/solution.py
@@ -9,17 +9,17 @@
 
 LN_EPS = 1e-6
 MESH = pl.DeviceIdType.MESH
-FC = 1024
-OWN_FIRST = 4
-LEAD = 4
-P_SLOTS = 3
-D_SLOTS = 4
+FC = 512
+OWN_FIRST = 8
+LEAD = 8
+P_SLOTS = 5
+D_SLOTS = 6
 L_SLOTS = LEAD + P_SLOTS
-HELD = 4
+HELD = 8
 RING = 16
-STAGES = (1, 2, 4, 6, 8, 9)
-W_SLOTS = 3
-VMEM_LIMIT = 49 * 1024 * 1024
+STAGES = (2, 4, 6, 8, 10, 12)
+W_SLOTS = 6
+VMEM_LIMIT = 48 * 1024 * 1024
 
 
 def contract_rows(left_op, right_op):

time: 190 us -> 199 us (1.047)
  Pallas kernels: 190 us -> 198 us
    pallas_call x1, Pallas kernels: 16.4 us -> 27.4 us  [local_step(): pl.pallas_call(weight_grad_kernel, out_shape=[S((dl, fl), f32)] * 2 + [S(...]
    pallas_call x1, Pallas kernels: 173 us -> 171 us  [local_step(): pl.pallas_call(functools.partial(branch_kernel, d_model, n), out_shape=[V...]
where the time goes in v10:
time: 199 us
  Pallas kernels  198 us (99%)
    pallas_call x1, Pallas kernels, local_step(): pl.pallas_call(functools.partial(branch_kernel, d_model, n), out_shape=[V...  171 us
    pallas_call x1, Pallas kernels, local_step(): pl.pallas_call(weight_grad_kernel, out_shape=[S((dl, fl), f32)] * 2 + [S(...  27.4 us

profile of v10, /device:TPU:0, one launch (start us, length us, event | category | flops | bytes accessed | tf_op | source)
XLA Modules:
  0.0 198.9 jit_solution(654757726273994259)
XLA Ops:
  0.6 170.8 %shard_map.109 = (bf16[16,2,256,768]{3,2,1,0:T(8,128)(2,1)S(1)}, bf16[512,256]{1,0:T(8,128)(2,1)S(1)}, bf16[256,512]{1,0:T(8,128)(2,1)S(1)}, bf16[128,512]{1,0:T...) custom-call(bf16[128,512]{1,0:T(8,128)(2,1)} %x_hbm.1, bf16[128,512]{1,0:T(8,128)(2,1)} %dy_hbm.1, ...), custom_call_target="tpu_custom_call" | custom-call | flops 12884901888 | bytes 37748736 | tf_op jit(solution)/shard_map/pallas_call | solution.py:528
  171.5 27.4 %shard_map.110 = (f32[512,8192]{1,0:T(8,128)}, f32[512,8192]{1,0:T(8,128)}, f32[8192,512]{1,0:T(8,128)}, bf16[128,512]{1,0:T(8,128)(2,1)}, bf16[128,512]{1,0:T(8,128)(2,1)}, /*index=5*/f32[1,512]{1,0:T(1,128)}) custom-call(bf16[16,2,256,768]{3,2,1,0:T(8,128)(2,1)S(1)} %get-tuple-element.18.gat, bf16[512,256]{1,0:T(8,128)(2,1)S(1)} %get-tuple-element.19.h_t, ...), custom_call_target="tpu_custom_call" | custom-call | flops 6442450944 | bytes 62914560 | tf_op jit(solution)/shard_map/pallas_call | solution.py:552

commit v11 on v9

--- a/solution.py
+++ b/solution.py
@@ -16,8 +16,9 @@
 L_SLOTS = LEAD + P_SLOTS
 HELD = 8
 RING = 16
-STAGES = (1, 3, 6, 9, 13, 14)
-W_SLOTS = 3
+STAGES = (1, 2, 4, 5, 7, 8)
+W_SLOTS = 2
+W_UNITS = 2
 VMEM_LIMIT = 48 * 1024 * 1024
 
 
@@ -463,16 +464,18 @@
 
 
 def weight_grad_kernel(gat, h_t, dy_ref, y_in, dx_in, dg_in,
-                       dwg_hbm, dwu_hbm, dwd_hbm, y_hbm, dx_hbm, dg_hbm, buf, bsem, ssem):
-    n_blocks, _, _, width = gat.shape
+                       dwg_hbm, dwu_hbm, dwd_hbm, y_hbm, dx_hbm, dg_hbm, buf, buf2, bsem, ssem):
+    n_f, _, _, width = gat.shape
+    n_blocks = n_f // W_UNITS
     half = width // 3
-    WB = 2 * half
+    wb = 2 * half * W_UNITS
 
     def out_copy(b, k):
-        cs = pl.ds(mo(b * WB, WB), WB)
+        cs = pl.ds(mo(b * wb, wb), wb)
         dst = (dwg_hbm.at[:, cs], dwu_hbm.at[:, cs], dwd_hbm.at[cs, :])[k]
         slot = lax.rem(b, W_SLOTS)
-        return pltpu.make_async_copy(buf.at[slot, k], dst, bsem.at[slot, k])
+        src = buf.at[slot, k] if k < 2 else buf2.at[slot]
+        return pltpu.make_async_copy(src, dst, bsem.at[slot, k])
 
     def block(b, carry):
         slot = lax.rem(b, W_SLOTS)
@@ -481,13 +484,14 @@
             def _():
                 out_copy(b - W_SLOTS, k).wait()
 
-            for r in range(2):
-                rs = slice(r * half, (r + 1) * half)
-                src = gat[b, r, :, (k + 1) % 3 * half:((k + 1) % 3 + 1) * half]
+            for q in range(2 * W_UNITS):
+                rs = slice(q * half, (q + 1) * half)
+                lane = (k + 1) % 3 * half
+                src = gat[b * W_UNITS + q // 2, q % 2, :, lane:lane + half]
                 if k < 2:
                     buf[slot, k, :, rs] = jnp.dot(h_t[...], src, preferred_element_type=jnp.float32)
                 else:
-                    buf[slot, k, rs, :] = contract_rows(src, dy_ref[...])
+                    buf2[slot, rs, :] = contract_rows(src, dy_ref[...])
             out_copy(b, k).start()
         return carry
 
@@ -555,7 +559,7 @@
             in_specs=[vm] * 6,
             out_specs=[anyspec] * 6,
             scratch_shapes=[
-                V((W_SLOTS, 3, dl, FC), f32), sem((W_SLOTS, 3)), sem((3,)),
+                V((W_SLOTS, 2, dl, FC * W_UNITS), f32), V((W_SLOTS, FC * W_UNITS, dl), f32), sem((W_SLOTS, 3)), sem((3,)),
             ],
             compiler_params=pltpu.CompilerParams(vmem_limit_bytes=VMEM_LIMIT),
             cost_estimate=pl.CostEstimate(flops=6 * tok * dl * fl, bytes_accessed=12 * dl * fl + 6 * tok * fl, transcendentals=0),

time: 190 us -> 187 us (0.984)
  Pallas kernels: 189 us -> 186 us
    pallas_call x1, Pallas kernels: 172 us -> 169 us  [local_step(): pl.pallas_call(functools.partial(branch_kernel, d_model, n), out_shape=[V...]
where the time goes in v11:
time: 187 us
  Pallas kernels  186 us (99%)
    pallas_call x1, Pallas kernels, local_step(): pl.pallas_call(functools.partial(branch_kernel, d_model, n), out_shape=[V...  169 us
    pallas_call x1, Pallas kernels, local_step(): pl.pallas_call(weight_grad_kernel, out_shape=[S((dl, fl), f32)] * 2 + [S(...  16.6 us

profile of v11, /device:TPU:0, one launch (start us, length us, event | category | flops | bytes accessed | tf_op | source)
XLA Modules:
  0.0 186.6 jit_solution(2628864922824896015)
XLA Ops:
  0.6 169.4 %shard_map.109 = (bf16[16,2,256,768]{3,2,1,0:T(8,128)(2,1)S(1)}, bf16[512,256]{1,0:T(8,128)(2,1)S(1)}, bf16[256,512]{1,0:T(8,128)(2,1)S(1)}, bf16[128,512]{1,0:T...) custom-call(bf16[128,512]{1,0:T(8,128)(2,1)} %x_hbm.1, bf16[128,512]{1,0:T(8,128)(2,1)} %dy_hbm.1, ...), custom_call_target="tpu_custom_call" | custom-call | flops 12884901888 | bytes 37748736 | tf_op jit(solution)/shard_map/pallas_call | solution.py:532
  170.1 16.6 %shard_map.110 = (f32[512,8192]{1,0:T(8,128)}, f32[512,8192]{1,0:T(8,128)}, f32[8192,512]{1,0:T(8,128)}, bf16[128,512]{1,0:T(8,128)(2,1)}, bf16[128,512]{1,0:T(8,128)(2,1)}, /*index=5*/f32[1,512]{1,0:T(1,128)}) custom-call(bf16[16,2,256,768]{3,2,1,0:T(8,128)(2,1)S(1)} %get-tuple-element.18.gat, bf16[512,256]{1,0:T(8,128)(2,1)S(1)} %get-tuple-element.19.h_t, ...), custom_call_target="tpu_custom_call" | custom-call | flops 6442450944 | bytes 62914560 | tf_op jit(solution)/shard_map/pallas_call | solution.py:556

commit v12 on v9

--- a/solution.py
+++ b/solution.py
@@ -16,7 +16,7 @@
 L_SLOTS = LEAD + P_SLOTS
 HELD = 8
 RING = 16
-STAGES = (1, 3, 6, 9, 13, 14)
+STAGES = (1, 3, 5, 7, 8, 9)
 W_SLOTS = 3
 VMEM_LIMIT = 48 * 1024 * 1024
 

time: 190 us -> 188 us (0.989)
  Pallas kernels: 189 us -> 187 us
where the time goes in v12:
time: 188 us
  Pallas kernels  187 us (99%)
    pallas_call x1, Pallas kernels, local_step(): pl.pallas_call(functools.partial(branch_kernel, d_model, n), out_shape=[V...  171 us
    pallas_call x1, Pallas kernels, local_step(): pl.pallas_call(weight_grad_kernel, out_shape=[S((dl, fl), f32)] * 2 + [S(...  16.4 us

profile of v12, /device:TPU:0, one launch (start us, length us, event | category | flops | bytes accessed | tf_op | source)
XLA Modules:
  0.0 187.8 jit_solution(17812372128637718529)
XLA Ops:
  0.6 170.8 %shard_map.109 = (bf16[16,2,256,768]{3,2,1,0:T(8,128)(2,1)S(1)}, bf16[512,256]{1,0:T(8,128)(2,1)S(1)}, bf16[256,512]{1,0:T(8,128)(2,1)S(1)}, bf16[128,512]{1,0:T...) custom-call(bf16[128,512]{1,0:T(8,128)(2,1)} %x_hbm.1, bf16[128,512]{1,0:T(8,128)(2,1)} %dy_hbm.1, ...), custom_call_target="tpu_custom_call" | custom-call | flops 12884901888 | bytes 37748736 | tf_op jit(solution)/shard_map/pallas_call | solution.py:528
  171.4 16.4 %shard_map.110 = (f32[512,8192]{1,0:T(8,128)}, f32[512,8192]{1,0:T(8,128)}, f32[8192,512]{1,0:T(8,128)}, bf16[128,512]{1,0:T(8,128)(2,1)}, bf16[128,512]{1,0:T(8,128)(2,1)}, /*index=5*/f32[1,512]{1,0:T(1,128)}) custom-call(bf16[16,2,256,768]{3,2,1,0:T(8,128)(2,1)S(1)} %get-tuple-element.18.gat, bf16[512,256]{1,0:T(8,128)(2,1)S(1)} %get-tuple-element.19.h_t, ...), custom_call_target="tpu_custom_call" | custom-call | flops 6442450944 | bytes 62914560 | tf_op jit(solution)/shard_map/pallas_call | solution.py:552

commit v13 on v7

--- a/solution.py
+++ b/solution.py
@@ -37,7 +37,7 @@
                   x_hbm, dy_hbm, gain_hbm, wg_hbm, wu_hbm, wd_hbm,
                   gat, h_t, dya_ref, y_ref, dx_ref, dg_ref,
                   x_ref, gain_ref, h_ref,
-                  wg, wu, wd, xh, part, part_d, dsum, dsum_d, r1, r2, acc, zin, st, rb, dgs, dgr,
+                  wg, wu, wd, xh, part, part_d, dsum, dsum_d, r1, r2, ga, acc, zin, st, rb, dgs, dgr,
                   wsem, isem, zs, zr, ss, sr, bs, br, ds, dr, dds, ddr, p1s, p1r, pds, pdr, p2s, p2r,
                   g1s, g1r, g2s, g2r, gds, gdr, a1s, a1r, a2s, a2r, ads, adr):
     half = FC // 2
@@ -194,17 +194,17 @@
         ref = gat.at[f_of(j), :, grows(j, off, q1), lo * half:]
         return remote(ref, ref, gds.at[ring(j)], gdr.at[ring(j)], dev_c)
 
-    def a1_copy(k, r, off):
-        ref = gat.at[f_of(held + k), r, grows(held + k, off[r], q3), lanes[0]]
-        return remote(ref, ref, a1s.at[r, k], a1r.at[r, k], dev2[r])
-
-    def a2_copy(k, r, off):
-        ref = gat.at[f_of(held + k), r, grows(held + k, off[r], q2), lanes[0]]
-        return remote(ref, ref, a2s.at[r, k], a2r.at[r, k], dev1[r])
-
-    def ad_copy(k, off):
-        ref = gat.at[f_of(held + k), :, grows(held + k, off, q1), lanes[0]]
-        return remote(ref, ref, ads.at[k], adr.at[k], dev_c)
+    def a1_copy(r, off):
+        ref = ga.at[r, seg(off[r], q3), :]
+        return remote(ref, ref, a1s.at[r], a1r.at[r], dev2[r])
+
+    def a2_copy(r, off):
+        ref = ga.at[r, seg(off[r], q2), :]
+        return remote(ref, ref, a2s.at[r], a2r.at[r], dev1[r])
+
+    def ad_copy(off):
+        ref = ga.at[:, seg(off, q1), :]
+        return remote(ref, ref, ads.at[0], adr.at[0], dev_c)
 
     def by_arrays(j, body):
         @pl.when(j < held)
@@ -356,7 +356,16 @@
                 swish = u * sig
                 f = f_of(j)
                 rs = grows(j, g_fin[r], q3)
-                gat[f, r, rs, lanes[0]] = (swish * v).astype(jnp.bfloat16)
+                act = (swish * v).astype(jnp.bfloat16)
+
+                @pl.when(j < held)
+                def _():
+                    gat[f, r, rs, lanes[0]] = act
+
+                @pl.when(j >= held)
+                def _():
+                    ga[r, seg(g_fin[r], q3), pl.ds(mo((j - held) * half, half), half)] = act
+
                 gat[f, r, rs, lanes[1]] = (da * v * sig * (1.0 + u * (1.0 - sig))).astype(jnp.bfloat16)
                 gat[f, r, rs, lanes[2]] = (da * swish).astype(jnp.bfloat16)
             by_arrays(j, lambda lo: [g1_copy(j, r, g_fin, lo).start() for r in range(2)])
@@ -413,16 +422,14 @@
 
         @pl.when(i == n_units - 1 + STAGES[2])
         def _():
-            each_held(lambda k: [a1_copy(k, r, g_fin).start() for r in range(2)])
+            for r in range(2):
+                a1_copy(r, g_fin).start()
 
         @pl.when(i == n_units - 1 + STAGES[3])
         def _():
-            def forward(k):
-                for r in range(2):
-                    a1_copy(k, r, g_fin_n).wait_recv()
-                    a2_copy(k, r, g_keep1).start()
-
-            each_held(forward)
+            for r in range(2):
+                a1_copy(r, g_fin_n).wait_recv()
+                a2_copy(r, g_keep1).start()
         return carry
 
     lax.fori_loop(0, n_units + STAGES[5], step, 0)
@@ -436,20 +443,21 @@
     z_dg = remote(dgs, dgr, zs.at[3], zr.at[3], dev_z)
     z_dg.start()
 
-    def to_core(k):
+    for r in range(2):
+        a2_copy(r, g_send1).wait_recv()
+    ad_copy(g_c[0]).start()
+    for r in range(2):
+        a1_copy(r, g_fin).wait_send()
+        a2_copy(r, g_keep1).wait_send()
+    ad_copy(g_c[1]).wait_recv()
+    ad_copy(g_c[0]).wait_send()
+
+    def m_product(k):
+        j = held + k
         for r in range(2):
-            a2_copy(k, r, g_send1).wait_recv()
-        ad_copy(k, g_c[0]).start()
-
-    each_held(to_core)
-
-    def m_product(k):
-        ad_copy(k, g_c[1]).wait_recv()
-        acc[0, 0] += m_part(f_of(held + k), own, held + k)
-        for r in range(2):
-            a1_copy(k, r, g_fin).wait_send()
-            a2_copy(k, r, g_keep1).wait_send()
-        ad_copy(k, g_c[0]).wait_send()
+            act = ga[r, :, pl.ds(mo(k * half, half), half)]
+            gat[f_of(j), r, own, lanes[0]] = act
+            acc[0, 0] += jnp.dot(act, wd[rcols(j, r), :], preferred_element_type=jnp.float32)
 
     each_held(m_product)
     y_ref[...] = (x_ref[...].astype(jnp.float32) + (acc[0, 0] + zin[0])).astype(jnp.bfloat16)
@@ -537,13 +545,14 @@
                 V((P_SLOTS, 2, 2, rows, half), f32), V((L_SLOTS, 2, rows, half), f32),
                 V((P_SLOTS, 2, 2, rows // 2, half), f32), V((L_SLOTS, 2, rows // 2, half), f32),
                 V((2 * n, 2, 3, rows // 4, half), f32), V((2 * n, 2, 3, rows // 8, half), f32),
+                V((2, rows, HELD * half), bf16),
                 V((2, 2, rows, dl), f32), V((2, rows, dl), f32),
                 V((8, 8, 128), f32), V((8, 8, 128), f32), V((8, dl), f32), V((8, dl), f32),
                 sem((3, n)), sem((3,)), sem((4,)), sem((4,)), sem((8,)), sem((8,)), sem((8,)), sem((8,)),
                 sem((RING,)), sem((RING,)), sem((RING,)), sem((RING,)),
                 *[sem((2, RING)) for _ in range(10)],
                 sem((RING,)), sem((RING,)),
-                *[sem((2, HELD)) for _ in range(4)], sem((HELD,)), sem((HELD,)),
+                *[sem((2,)) for _ in range(4)], sem((1,)), sem((1,)),
             ],
             compiler_params=pltpu.CompilerParams(collective_id=0, has_side_effects=True, vmem_limit_bytes=VMEM_LIMIT),
             cost_estimate=pl.CostEstimate(flops=12 * tok * dl * fl, bytes_accessed=6 * dl * fl + 6 * tok * fl, transcendentals=0),

time: 185 us -> 186 us (level)
  no operation moved by 1% of the time
where the time goes in v13:
time: 186 us
  Pallas kernels  185 us (99%)
    pallas_call x1, Pallas kernels, local_step(): pl.pallas_call(functools.partial(branch_kernel, d_model, n), out_shape=[V...  169 us
    pallas_call x1, Pallas kernels, local_step(): pl.pallas_call(weight_grad_kernel, out_shape=[S((dl, fl), f32)] * 2 + [S(...  16.4 us

profile of v13, /device:TPU:0, one launch (start us, length us, event | category | flops | bytes accessed | tf_op | source)
XLA Modules:
  0.0 185.8 jit_solution(8982618383670266878)
XLA Ops:
  0.6 168.8 %shard_map.109 = (bf16[16,2,256,768]{3,2,1,0:T(8,128)(2,1)S(1)}, bf16[512,256]{1,0:T(8,128)(2,1)S(1)}, bf16[256,512]{1,0:T(8,128)(2,1)S(1)}, bf16[128,512]{1,0:T...) custom-call(bf16[128,512]{1,0:T(8,128)(2,1)} %x_hbm.1, bf16[128,512]{1,0:T(8,128)(2,1)} %dy_hbm.1, ...), custom_call_target="tpu_custom_call" | custom-call | flops 12884901888 | bytes 37748736 | tf_op jit(solution)/shard_map/pallas_call | solution.py:536
  169.4 16.4 %shard_map.110 = (f32[512,8192]{1,0:T(8,128)}, f32[512,8192]{1,0:T(8,128)}, f32[8192,512]{1,0:T(8,128)}, bf16[128,512]{1,0:T(8,128)(2,1)}, bf16[128,512]{1,0:T(8,128)(2,1)}, /*index=5*/f32[1,512]{1,0:T(1,128)}) custom-call(bf16[16,2,256,768]{3,2,1,0:T(8,128)(2,1)S(1)} %get-tuple-element.18.gat, bf16[512,256]{1,0:T(8,128)(2,1)S(1)} %get-tuple-element.19.h_t, ...), custom_call_target="tpu_custom_call" | custom-call | flops 6442450944 | bytes 62914560 | tf_op jit(solution)/shard_map/pallas_call | solution.py:561

commit v14 on v5

--- a/solution.py
+++ b/solution.py
@@ -14,11 +14,11 @@
 LEAD = 8
 P_SLOTS = 4
 L_SLOTS = LEAD + P_SLOTS
-HELD = 8
+HELD = 6
 RING = 16
 STAGES = (1, 3, 5, 7, 9, 10)
 WB = 512
-W_SLOTS = 3
+W_SLOTS = 4
 VMEM_LIMIT = 48 * 1024 * 1024
 
 

time: 185 us -> 185 us (level)
  no operation moved by 1% of the time
where the time goes in v14:
time: 185 us
  Pallas kernels  184 us (99%)
    pallas_call x1, Pallas kernels, local_step(): pl.pallas_call(functools.partial(branch_kernel, d_model, n), out_shape=[V...  168 us
    pallas_call x1, Pallas kernels, local_step(): pl.pallas_call(weight_grad_kernel, out_shape=[S((dl, fl), f32)] * 2 + [S(...  16.4 us

profile of v14, /device:TPU:0, one launch (start us, length us, event | category | flops | bytes accessed | tf_op | source)
XLA Modules:
  0.0 185.1 jit_solution(15827596869457657675)
XLA Ops:
  0.6 168.0 %shard_map.109 = (bf16[3,256,8192]{2,1,0:T(8,128)(2,1)S(1)}, bf16[512,256]{1,0:T(8,128)(2,1)S(1)}, bf16[256,512]{1,0:T(8,128)(2,1)S(1)}, bf16[128,512]{1,0:T(8,1...) custom-call(bf16[128,512]{1,0:T(8,128)(2,1)} %x_hbm.1, bf16[128,512]{1,0:T(8,128)(2,1)} %dy_hbm.1, ...), custom_call_target="tpu_custom_call" | custom-call | flops 12884901888 | bytes 37748736 | tf_op jit(solution)/shard_map/pallas_call | solution.py:521
  168.6 16.4 %shard_map.110 = (f32[512,8192]{1,0:T(8,128)}, f32[512,8192]{1,0:T(8,128)}, f32[8192,512]{1,0:T(8,128)}, bf16[128,512]{1,0:T(8,128)(2,1)}, bf16[128,512]{1,0:T(8,128)(2,1)}, /*index=5*/f32[1,512]{1,0:T(1,128)}) custom-call(bf16[3,256,8192]{2,1,0:T(8,128)(2,1)S(1)} %get-tuple-element.18.gat, bf16[512,256]{1,0:T(8,128)(2,1)S(1)} %get-tuple-element.19.h_t, ...), custom_call_target="tpu_custom_call" | custom-call | flops 6442450944 | bytes 62914560 | tf_op jit(solution)/shard_map/pallas_call | solution.py:545
